TPU v7x, 64 devices: a 2x2x8 block of a 4x4x8 slice. The times are simulated.
64 devices in a mesh: dp: 4 (over x, y), sp: 16 (over z, core).
Axes of the slice: x: 2, y: 2, z: 8, core: 2. Of those that a mesh axis runs over, the one named last changes fastest.
The devices are a block of a 4x4x8 slice.
Arguments:
- x: bfloat16 [32768, 4096], P(('dp', 'sp')), parts along dimension 0
- doc_start: int32 [32768], P(('dp', 'sp')), parts along dimension 0
- w_in: bfloat16 [4096, 18560], replicated
- conv_w: float32 [4, 10240], replicated
- conv_b: float32 [10240], replicated
- dt_bias: float32 [128], replicated
- a_log: float32 [128], replicated
- d_skip: float32 [128], replicated
- norm_w: float32 [8, 1024], replicated
- w_out: bfloat16 [8192, 4096], replicated
Outputs:
- output: bfloat16 [32768, 4096], P(('dp', 'sp')), parts along dimension 0
There are 4 independent parts. A program takes and returns all parts, laid end to end along the dimension named above; an argument that names none is the same for every part.
All inputs are finite; a program needn't handle non-finite values.
Results may differ from a plain program's by a relative error of at most 0.00217803.
Values are sent between devices in bfloat16 or wider.
A program may use at most 768 MiB of HBM per device.

v0:
```python
import math
import jax
import jax.numpy as jnp
from jax import lax
from jax.sharding import PartitionSpec as P

CHUNK_LEN = 256
NORM_EPS = 1e-5


def conv_halo_rows(conv_in, keep_flag, conv_width):
    n_tok = conv_in.shape[0]
    tail_keep = jnp.cumprod(keep_flag[n_tok - conv_width + 2:][::-1])[::-1]
    tail_ok = jnp.concatenate([tail_keep, jnp.ones((1,), jnp.float32)])
    last_rows = conv_in[n_tok - conv_width + 1:]
    return jnp.where(tail_ok[:, None] > 0.5, last_rows, jnp.zeros_like(last_rows))


def causal_conv(conv_in, halo_rows, keep_flag, conv_w, conv_b):
    conv_width = conv_w.shape[0]
    n_tok = conv_in.shape[0]
    ext_rows = jnp.concatenate([halo_rows, conv_in], axis=0)
    keep_ext = jnp.concatenate([jnp.ones((conv_width - 1,), jnp.float32), keep_flag])
    pre_act = conv_b + conv_w[0] * conv_in
    tap_mask = jnp.ones((n_tok,), jnp.float32)
    for offset in range(1, conv_width):
        tap_mask = tap_mask * keep_ext[conv_width - offset:conv_width - offset + n_tok]
        pre_act = pre_act + conv_w[offset] * (tap_mask[:, None] * ext_rows[conv_width - 1 - offset:conv_width - 1 - offset + n_tok])
    return jax.nn.silu(pre_act).astype(jnp.bfloat16)


def local_scan(conv_out, dt_val, doc_start, a_log, groups, d_inner):
    n_tok = conv_out.shape[0]
    n_heads = a_log.shape[0]
    per_group = n_heads // groups
    head_dim = d_inner // n_heads
    state_dim = (conv_out.shape[1] - d_inner) // (2 * groups)
    n_chunks = n_tok // CHUNK_LEN
    xs_chunk = conv_out[:, :d_inner].reshape(n_chunks, CHUNK_LEN, groups, per_group, head_dim)
    b_chunk = conv_out[:, d_inner:d_inner + groups * state_dim].reshape(n_chunks, CHUNK_LEN, groups, state_dim)
    c_chunk = conv_out[:, d_inner + groups * state_dim:].reshape(n_chunks, CHUNK_LEN, groups, state_dim)
    dt_chunk = dt_val.reshape(n_chunks, CHUNK_LEN, groups, per_group)
    cum_decay = jnp.cumsum(-jnp.exp(a_log).reshape(groups, per_group) * dt_chunk, axis=1)
    seg_ids = jnp.cumsum(doc_start.reshape(n_chunks, CHUNK_LEN), axis=1)
    position = jnp.arange(CHUNK_LEN)
    allowed = (position[:, None] >= position[None, :]) & (seg_ids[:, :, None] == seg_ids[:, None, :])
    cum_rows = jnp.moveaxis(cum_decay, 1, -1)
    decay_mat = jnp.exp(jnp.where(allowed[:, None, None], cum_rows[..., :, None] - cum_rows[..., None, :], -jnp.inf))
    scores = jnp.einsum('cign,cjgn->cgij', c_chunk, b_chunk, preferred_element_type=jnp.float32)
    mix_mat = (scores[:, :, None] * decay_mat * jnp.moveaxis(dt_chunk, 1, -1)[..., None, :]).astype(jnp.bfloat16)
    y_intra = jnp.einsum('cgkij,cjgkp->cigkp', mix_mat, xs_chunk, preferred_element_type=jnp.float32)
    last_cum = cum_decay[:, -1]
    end_same = seg_ids == seg_ids[:, -1:]
    w_end = jnp.exp(last_cum[:, None] - cum_decay) * dt_chunk * end_same[..., None, None]
    scaled_x = (xs_chunk * w_end[..., None]).astype(jnp.bfloat16)
    chunk_state = jnp.einsum('cjgkp,cjgn->cgkpn', scaled_x, b_chunk, preferred_element_type=jnp.float32)
    chunk_reset = (seg_ids[:, -1] > 0).astype(jnp.int32)
    chunk_decay = jnp.exp(last_cum) * (chunk_reset == 0)[:, None, None]
    cum_in = jnp.cumsum(last_cum, axis=0)
    cum_ex = cum_in - last_cum
    reset_in = jnp.cumsum(chunk_reset)
    reset_ex = reset_in - chunk_reset
    chunk_idx = jnp.arange(n_chunks)
    link_ok = (chunk_idx[:, None] > chunk_idx[None, :]) & (reset_ex[:, None] == reset_in[None, :])
    carry_w = jnp.exp(jnp.where(link_ok[:, :, None, None], cum_ex[:, None] - cum_in[None, :], -jnp.inf))
    local_start = jnp.einsum('cdgk,dgkpn->cgkpn', carry_w, chunk_state, precision=lax.Precision.HIGHEST)
    start_decay = jnp.exp(cum_ex) * (reset_ex == 0)[:, None, None]
    w_start = jnp.exp(cum_decay) * (seg_ids == 0)[..., None, None]
    return y_intra, local_start, start_decay, w_start, c_chunk, chunk_state, chunk_decay


def finish_layer(y_intra, local_start, start_decay, w_start, c_chunk, state_in, conv_out, gate_in, d_skip, norm_w, w_out):
    n_tok = conv_out.shape[0]
    n_heads = d_skip.shape[0]
    groups, group_width = norm_w.shape
    d_inner = groups * group_width
    head_dim = d_inner // n_heads
    start_states = local_start + start_decay[..., None, None] * state_in
    y_state = jnp.einsum('cign,cgkpn->cigkp', c_chunk, start_states.astype(jnp.bfloat16), preferred_element_type=jnp.float32) * w_start[..., None]
    y_heads = (y_intra + y_state).reshape(n_tok, n_heads, head_dim) + d_skip[:, None] * conv_out[:, :d_inner].reshape(n_tok, n_heads, head_dim)
    gated_y = y_heads.reshape(n_tok, groups, group_width) * jax.nn.silu(gate_in.astype(jnp.float32)).reshape(n_tok, groups, group_width)
    normed = gated_y * lax.rsqrt(jnp.mean(gated_y * gated_y, axis=-1, keepdims=True) + NORM_EPS) * norm_w
    return jnp.dot(normed.reshape(n_tok, d_inner).astype(jnp.bfloat16), w_out, preferred_element_type=jnp.float32).astype(jnp.bfloat16)


def solution(mesh):
    n_seq = mesh.shape['sp']
    n_rounds = int(math.ceil(math.log2(n_seq)))
    next_pairs = [(source, source + 1) for source in range(n_seq - 1)]
    row_spec = P(('dp', 'sp'), None)
    tok_spec = P(('dp', 'sp'))

    def layer_shard(x, doc_start, w_in, conv_w, conv_b, dt_bias, a_log, d_skip, norm_w, w_out):
        groups = norm_w.shape[0]
        d_inner = norm_w.shape[0] * norm_w.shape[1]
        conv_dim = conv_w.shape[1]
        seq_rank = lax.axis_index('sp')
        projected = jnp.dot(x, w_in, preferred_element_type=jnp.float32).astype(jnp.bfloat16)
        conv_in = projected[:, d_inner:d_inner + conv_dim]
        keep_flag = (1 - doc_start).astype(jnp.float32)
        halo_rows = lax.ppermute(conv_halo_rows(conv_in, keep_flag, conv_w.shape[0]), 'sp', next_pairs)
        conv_out = causal_conv(conv_in, halo_rows, keep_flag, conv_w, conv_b)
        dt_val = jax.nn.softplus(projected[:, d_inner + conv_dim:].astype(jnp.float32) + dt_bias)
        pieces = local_scan(conv_out, dt_val, doc_start, a_log, groups, d_inner)
        y_intra, local_start, start_decay, w_start, c_chunk, chunk_state, chunk_decay = pieces
        acc_decay = start_decay[-1] * chunk_decay[-1]
        acc_state = chunk_decay[-1][..., None, None] * local_start[-1] + chunk_state[-1]
        for round_idx in range(n_rounds):
            hop_len = 2 ** round_idx
            hop_pairs = [(source, source + hop_len) for source in range(n_seq - hop_len)]
            got_decay = lax.ppermute(acc_decay, 'sp', hop_pairs)
            got_state = lax.ppermute(acc_state, 'sp', hop_pairs)
            got_decay = jnp.where(seq_rank >= hop_len, got_decay, 1.0)
            acc_state = acc_decay[..., None, None] * got_state + acc_state
            acc_decay = got_decay * acc_decay
        state_in = lax.ppermute(acc_state, 'sp', next_pairs)
        return finish_layer(y_intra, local_start, start_decay, w_start, c_chunk, state_in, conv_out, projected[:, :d_inner], d_skip, norm_w, w_out)

    return jax.shard_map(layer_shard, mesh=mesh, in_specs=(row_spec, tok_spec, P(), P(), P(), P(), P(), P(), P(), P()), out_specs=row_spec, check_vma=False)
```

profile of v0, /device:TPU:21, one launch (start us, length us, event | category | flops | bytes accessed | tf_op | source)
XLA Modules:
  0.0 1092.6 jit_solution(136006624415370909)
XLA Ops:
  2.3 92.6 %convolution_convert_fusion = bf16[512,18560]{1,0:T(8,128)(2,1)} fusion(bf16[512,4096]{1,0:T(8,128)(2,1)} %param.10, bf16[4096,18560]{1,0:T(8,128)(2,1)} %param.12), kind=kOutput, calls=%fused_computation.8 | convolution fusion | flops 77855784960 | bytes 175243264 | tf_op jit(solution)/shard_map/dot_general | solution.py:98
  95.9 5.6 collective-permute-start
  103.1 1.1 compare_select_fusion
  104.6 2.0 copy.125
  106.9 18.0 %reduce-window.37 = f32[2,16,8,2,128]{4,2,3,1,0:T(8,128)S(1)} reduce-window(f32[2,16,8,2,128]{4,2,3,1,0:T(8,128)S(1)} %bitcast.138, f32[]{:T(128)} %constant.29.clone.1), window={size=1x1x1x1x128 pad=0_0x0_0x0_0x0_0x127_0}, to_apply=%region_3.4 | reduce-window | flops 8323072 | bytes 524292 | tf_op jit(solution)/shard_map/reduce-window.3
  128.9 4.8 multiply_multiply_fusion
  133.8 9.3 slice.115
  144.1 25.4 %multiply_convert_fusion.2 = bf16[512,10240]{1,0:T(8,128)(2,1)S(1)} fusion(bf16[512,10240]{1,0:T(8,128)(2,1)} %slice.115, bf16[3,10240]{1,0:T(4,128)(2,1)S(1)} %collective-permute-done, f32[512]{0:T(512)S(1)} %get-tuple-element.7, f32[10240]{0:T(1024)S(1)} %bitcast.141, f32[512]{0:T(512)S(1)} %get-tuple-element.8, f32[10240]{0:T(1024)S(1)} %bitcast.142, ...), kind=kLoop, calls=%fused_computation.11 | loop fusion | flops 152043520 | bytes 21243904 | tf_op jit(solution)/shard_map/convert_element_type | solution.py:29
  169.4 9.4 slice_convert_fusion
  178.8 1.9 copy-done.1
  180.8 1.2 slice_bitcast_fusion.3
  182.0 11.9 %copy.113 = bf16[512,8192]{0,1:T(8,128)(2,1)} copy(bf16[512,8192]{1,0:T(8,128)(2,1)} %get-tuple-element.10) | data formatting | bytes 16777216 | tf_op jit(solution)/shard_map/slice | solution.py:39
  193.9 12.5 %reshape.296 = bf16[2,256,8,16,64]{1,0,4,3,2:T(2,128)(2,1)} reshape(bf16[512,8192]{0,1:T(8,128)(2,1)} %copy.113) | data formatting | bytes 16777216 | tf_op jit(solution)/shard_map/reshape | solution.py:39
  206.8 8.9 multiply_convert_fusion.4
  215.6 5.7 fusion.14
  221.3 32.0 %fusion.19 = f32[8,16,64,128,2]{3,4,2,1,0:T(2,128)S(1)} fusion(f32[2,8,16,64,128]{4,3,2,1,0:T(8,128)S(1)} %fusion.14, pred[2,2]{1,0:T(4,128)(4,1)S(1)} %compare_and_fusion.1, f32[2,8,16]{0,2,1:T(8,128)S(1)} %copy.132, f32[2,8,16]{0,2,1:T(8,128)S(1)} %copy.131), kind=kOutput, calls=%fused_computation.33 | convolution fusion | flops 50332672 | bytes 16779268 | tf_op jit(solution)/shard_map/cdgk,dgkpn->cgkpn/dot_general | solution.py:66
  253.4 4.8 copy.186
  258.2 3.2 fusion.22
  261.4 2.0 collective-permute-start.4
  263.4 45.4 %collective-permute-done.4 = f32[8,16,64,128]{3,2,1,0:T(8,128)S(1)} collective-permute-done((f32[8,16,64,128]{3,2,1,0:T(8,128)S(1)}, f32[8,16,64,128]{3,2,1,0:T(8,128)S(1)}, u32[]{:S(2)}, u32[]{:S(2)}) %collective-permute-start.4) | collective-permute-done | bytes 4194336 | tf_op jit(solution)/shard_map/ppermute | solution.py:112
  308.8 2.7 multiply_add_fusion.3
  311.5 5.7 collective-permute-start.5
  317.2 2.8 collective-permute-start.1
  320.0 84.5 %collective-permute-done.1 = f32[8,16]{1,0:T(8,128)S(1)} collective-permute-done((f32[8,16]{1,0:T(8,128)S(1)}, f32[8,16]{1,0:T(8,128)S(1)}, u32[]{:S(2)}, u32[]{:S(2)}) %collective-permute-start.1) | collective-permute-done | bytes 544 | tf_op jit(solution)/shard_map/ppermute | solution.py:111
  404.5 6.0 multiply_add_fusion.2
  410.4 9.7 collective-permute-start.6
  420.1 4.2 collective-permute-start.2
  424.3 83.8 %collective-permute-done.2 = f32[8,16]{1,0:T(8,128)S(1)} collective-permute-done((f32[8,16]{1,0:T(8,128)S(1)}, f32[8,16]{1,0:T(8,128)S(1)}, u32[]{:S(2)}, u32[]{:S(2)}) %collective-permute-start.2) | collective-permute-done | bytes 544 | tf_op jit(solution)/shard_map/ppermute | solution.py:111
  508.1 6.0 multiply_add_fusion.1
  514.1 98.9 %collective-permute-start.7 = (f32[8,16,64,128]{3,2,1,0:T(8,128)}, f32[8,16,64,128]{3,2,1,0:T(8,128)}, u32[]{:S(2)}, u32[]{:S(2)}) collective-permute-start(f32[8,16,64,128]{3,2,1,0:T(8,128)} %multiply_add_fusion.1), channel_id=1, source_target_pairs={{0,8},{1,9},{2,10},{3,11},{4,12},{5,13},{6,14},{7,15},{16,24},{17,... | collective-permute-start | bytes 12582920 | tf_op jit(solution)/shard_map/ppermute | solution.py:112
  612.9 1.5 collective-permute-start.3
  614.5 86.6 %collective-permute-done.3 = f32[8,16]{1,0:T(8,128)S(1)} collective-permute-done((f32[8,16]{1,0:T(8,128)S(1)}, f32[8,16]{1,0:T(8,128)S(1)}, u32[]{:S(2)}, u32[]{:S(2)}) %collective-permute-start.3) | collective-permute-done | bytes 544 | tf_op jit(solution)/shard_map/ppermute | solution.py:111
  701.0 6.1 multiply_add_fusion
  707.1 91.5 %collective-permute-start.8 = (f32[8,16,64,128]{3,2,1,0:T(8,128)}, f32[8,16,64,128]{3,2,1,0:T(8,128)}, u32[]{:S(2)}, u32[]{:S(2)}) collective-permute-start(f32[8,16,64,128]{3,2,1,0:T(8,128)} %multiply_add_fusion), channel_id=1, source_target_pairs={{0,1},{1,2},{2,3},{3,4},{4,5},{5,6},{6,7},{7,8},{8,9},{9,10},{10,1... | collective-permute-start | bytes 12582920 | tf_op jit(solution)/shard_map/ppermute | solution.py:116
  798.6 11.0 %convert_multiply_fusion = f32[512,8192]{1,0:T(8,128)} fusion(bf16[512,18560]{1,0:T(8,128)(2,1)} %convolution_convert_fusion), kind=kLoop, calls=%fused_computation.9 | loop fusion | flops 20971520 | bytes 25165824 | tf_op jit(solution)/shard_map/jit(silu)/mul | solution.py:81
  810.6 1.7 copy.120
  813.7 17.6 %copy.152 = f32[512,8192]{0,1:T(8,128)} copy(f32[512,8192]{1,0:T(8,128)} %convert_multiply_fusion) | data formatting | bytes 33554432 | tf_op jit(solution)/shard_map/reshape | solution.py:81
  833.0 17.5 %copy.151 = f32[512,8192]{0,1:T(8,128)} copy(f32[512,8192]{1,0:T(8,128)} %get-tuple-element.9) | data formatting | bytes 33554432 | tf_op jit(solution)/shard_map/convert_element_type | solution.py:80
  851.3 25.7 %fusion = f32[2,8,16,64,256]{4,3,2,1,0:T(8,128)} fusion(f32[2,8,16,256]{3,2,1,0:T(8,128)} %copy.122, f32[2,8,16,256]{3,2,1,0:T(8,128)} %copy.120, f32[2,8,256,256]{3,2,1,0:T(8,128)S(1)} %fusion.29, pred[2,256,256]{2,1,0:T(8,128)(4,1)} %compare_and_fusion, bf16[2,256,8,16,64]{1,0,4,3,2:T(2,128)(2,1)} %reshape.296), kind=kOutput, calls=%fused_computation.1 | convolution fusion | flops 2231369728 | bytes 30015488 | tf_op jit(solution)/shard_map/cgkij,cjgkp->cigkp/dot_general | solution.py:51
  877.0 17.4 %fusion.10 = f32[2,256,8,16,64]{1,4,3,2,0:T(8,128)} fusion(f32[2,8,16,64,256]{4,3,2,1,0:T(8,128)} %fusion, f32[2,256,8,16]{1,3,2,0:T(8,128)S(1)} %copy.136, f32[8,16,64,128]{3,2,1,0:T(8,128)} %collective-permute-done.8, f32[2,8,16]{2,1,0:T(8,128)S(1)} %copy-done.7, bf16[2,256,8,128,1]{3,2,1,0,4:T(8,128)(2,1)S(1)} %bitcast_bitcast_fusion.1, ...), kind=kOutput, calls=%fused_computation.16 | convolution fusion | flops 1088421888 | bytes 47449088 | tf_op jit(solution)/shard_map/cign,cgkpn->cigkp/dot_general | solution.py:79
  894.4 28.6 %copy.137 = f32[2,256,8,16,64]{1,0,4,3,2:T(2,128)} copy(f32[2,256,8,16,64]{1,4,3,2,0:T(8,128)} %fusion.10) | data formatting | bytes 33554432 | tf_op jit(solution)/shard_map/add | solution.py:80
  923.1 30.5 %copy.150 = f32[2,256,8,16,64]{4,3,2,1,0:T(8,128)} copy(f32[2,256,8,16,64]{1,4,3,2,0:T(8,128)} %fusion.10) | data formatting | bytes 33554432 | tf_op jit(solution)/shard_map/reshape | solution.py:80
  953.6 21.6 %reshape.305 = f32[512,8,1024]{0,2,1:T(8,128)} reshape(f32[2,256,8,16,64]{1,0,4,3,2:T(2,128)} %copy.137) | data formatting | bytes 33554432 | tf_op jit(solution)/shard_map/reshape | solution.py:80
  975.2 16.8 %multiply_reduce_fusion = f32[512,8]{0,1:T(8,128)S(1)} fusion(f32[512,8,1024]{0,2,1:T(8,128)} %reshape.305, f32[8,1024]{1,0:T(8,128)S(1)} %mul.345, f32[512,8192]{0,1:T(8,128)} %copy.152, f32[512,8192]{0,1:T(8,128)} %copy.151), kind=kLoop, calls=%fused_computation.18 | loop fusion | flops 20967424 | bytes 50380800 | tf_op jit(solution)/shard_map/reduce_sum | solution.py:82
  992.1 1.1 mul.350
  993.3 17.8 %copy.158 = f32[64,8,8,1024]{3,1,2,0:T(8,128)} copy(f32[64,8,8,1024]{3,2,1,0:T(8,128)S(1)} %bitcast.128) | data formatting | bytes 33554432
  1011.1 27.9 %reshape.311 = f32[512,8192]{1,0:T(8,128)} reshape(f32[2,256,8,16,64]{4,3,2,1,0:T(8,128)} %copy.150) | data formatting | bytes 33554432 | tf_op jit(solution)/shard_map/reshape | solution.py:80
  1039.0 53.4 %fusion.21 = bf16[512,4096]{1,0:T(8,128)(2,1)} fusion(bf16[8192,4096]{1,0:T(8,128)(2,1)} %param.19, f32[512,8192]{1,0:T(8,128)} %bitcast.130, f32[512,8192]{1,0:T(8,128)} %reshape.311, f32[8192]{0:T(1024)S(1)} %bitcast.144, f32[8192]{0:T(1024)S(1)} %copy-done.9, bf16[512,10240]{1,0:T(8,128)(2,1)} %copy-done.1, bf16[512,18560]{1,0:T(8,128)(2,1)} %convolution_convert_fusion), kind=kOutput, calls=%fused_computation.35 | convolution fusion | flops 34412167168 | bytes 121700352 | tf_op jit(solution)/shard_map/dot_general | solution.py:83
  (103 shorter events, 15.9 us)
Async XLA Ops:
  0.7 0.6 copy-start.12
  2.2 92.6 %copy-start.18 = (f32[2]{0:T(128)S(1)}, f32[2]{0:T(128)}, u32[]{:S(2)}) copy-start(f32[2]{0:T(128)} %rev.7) | copy-start | bytes 28
  2.2 99.3 %copy-start.13 = (f32[512]{0:T(512)S(1)}, f32[512]{0:T(512)}, u32[]{:S(2)}) copy-start(f32[512]{0:T(512)} %copy-done.12) | copy-start | bytes 6148
  2.2 99.4 %copy-start.14 = (s32[512]{0:T(512)S(1)}, s32[512]{0:T(512)}, u32[]{:S(2)}) copy-start(s32[512]{0:T(512)} %param.11) | copy-start | bytes 6148
  2.2 100.9 %copy-start.15 = (f32[128]{0:T(128)S(1)}, f32[128]{0:T(128)}, u32[]{:S(2)}) copy-start(f32[128]{0:T(128)} %param.15) | copy-start | bytes 1540
  2.2 102.3 %copy-start.17 = (f32[128]{0:T(128)S(1)}, f32[128]{0:T(128)}, u32[]{:S(2)}) copy-start(f32[128]{0:T(128)} %param.16) | copy-start | bytes 1540
  2.3 125.9 %copy-start.5 = (f32[4,10240]{1,0:T(4,128)S(1)}, f32[4,10240]{1,0:T(4,128)}, u32[]{:S(2)}) copy-start(f32[4,10240]{1,0:T(4,128)} %param.13) | copy-start | bytes 491524
  95.9 48.1 %collective-permute-start = (bf16[3,10240]{1,0:T(4,128)(2,1)S(1)}, bf16[3,10240]{1,0:T(4,128)(2,1)S(1)}, u32[]{:S(2)}, u32[]{:S(2)}) collective-permute-start(bf16[3,10240]{1,0:T(4,128)(2,1)S(1)} %slice_select_fusion), channel_id=1, source_target_pairs={{0,1},{1,2},{2,3},{3,4},{4,5},{5,6},{6,7},{7,8},{8,9},{9,10},{10,1... | collective-permute-start | bytes 184328 | tf_op jit(solution)/shard_map/ppermute | solution.py:101
  126.4 17.6 %copy-start.8 = (f32[10240]{0:T(1024)S(1)}, f32[10240]{0:T(1024)}, u32[]{:S(2)}) copy-start(f32[10240]{0:T(1024)} %param.14) | copy-start | bytes 122884
  127.4 16.6 %copy-start.6 = (f32[2,8,16]{2,1,0:T(8,128)}, f32[2,8,16]{2,1,0:T(8,128)S(1)}, u32[]{:S(2)}) copy-start(f32[2,8,16]{2,1,0:T(8,128)S(1)} %get-tuple-element.27) | copy-start | bytes 3076
  133.7 9.5 copy-start.3
  169.4 11.4 %copy-start.1 = (bf16[512,10240]{1,0:T(8,128)(2,1)}, bf16[512,10240]{1,0:T(8,128)(2,1)S(1)}, u32[]{:S(2)}) copy-start(bf16[512,10240]{1,0:T(8,128)(2,1)S(1)} %multiply_convert_fusion.2) | copy-start | bytes 31457284
  253.3 58.1 %copy-start = (f32[8,16,64,128,2]{3,4,2,1,0:T(2,128)}, f32[8,16,64,128,2]{3,4,2,1,0:T(2,128)S(1)}, u32[]{:S(2)}) copy-start(f32[8,16,64,128,2]{3,4,2,1,0:T(2,128)S(1)} %fusion.19) | copy-start | bytes 25165828
  261.4 47.4 %collective-permute-start.4 = (f32[8,16,64,128]{3,2,1,0:T(8,128)S(1)}, f32[8,16,64,128]{3,2,1,0:T(8,128)S(1)}, u32[]{:S(2)}, u32[]{:S(2)}) collective-permute-start(f32[8,16,64,128]{3,2,1,0:T(8,128)S(1)} %fusion.22), channel_id=1, source_target_pairs={{0,1},{1,2},{2,3},{3,4},{4,5},{5,6},{6,7},{7,8},{8,9},{9,10},{10,1... | collective-permute-start | bytes 12582920 | tf_op jit(solution)/shard_map/ppermute | solution.py:112
  311.5 93.0 %collective-permute-start.5 = (f32[8,16,64,128]{3,2,1,0:T(8,128)}, f32[8,16,64,128]{3,2,1,0:T(8,128)}, u32[]{:S(2)}, u32[]{:S(2)}) collective-permute-start(f32[8,16,64,128]{3,2,1,0:T(8,128)} %multiply_add_fusion.3), channel_id=1, source_target_pairs={{0,2},{1,3},{2,4},{3,5},{4,6},{5,7},{6,8},{7,9},{8,10},{9,11},{10,... | collective-permute-start | bytes 12582920 | tf_op jit(solution)/shard_map/ppermute | solution.py:112
  317.2 87.3 %collective-permute-start.1 = (f32[8,16]{1,0:T(8,128)S(1)}, f32[8,16]{1,0:T(8,128)S(1)}, u32[]{:S(2)}, u32[]{:S(2)}) collective-permute-start(f32[8,16]{1,0:T(8,128)S(1)} %get-tuple-element.5), channel_id=1, source_target_pairs={{0,1},{1,2},{2,3},{3,4},{4,5},{5,6},{6,7},{7,8},{8,9},{9,10},{10,1... | collective-permute-start | bytes 1544 | tf_op jit(solution)/shard_map/ppermute | solution.py:111
  410.4 97.7 %collective-permute-start.6 = (f32[8,16,64,128]{3,2,1,0:T(8,128)}, f32[8,16,64,128]{3,2,1,0:T(8,128)}, u32[]{:S(2)}, u32[]{:S(2)}) collective-permute-start(f32[8,16,64,128]{3,2,1,0:T(8,128)} %multiply_add_fusion.2), channel_id=1, source_target_pairs={{0,4},{1,5},{2,6},{3,7},{4,8},{5,9},{6,10},{7,11},{8,12},{9,13},{1... | collective-permute-start | bytes 12582920 | tf_op jit(solution)/shard_map/ppermute | solution.py:112
  420.1 88.0 %collective-permute-start.2 = (f32[8,16]{1,0:T(8,128)S(1)}, f32[8,16]{1,0:T(8,128)S(1)}, u32[]{:S(2)}, u32[]{:S(2)}) collective-permute-start(f32[8,16]{1,0:T(8,128)S(1)} %select_multiply_fusion.2), channel_id=1, source_target_pairs={{0,2},{1,3},{2,4},{3,5},{4,6},{5,7},{6,8},{7,9},{8,10},{9,11},{10,... | collective-permute-start | bytes 1544 | tf_op jit(solution)/shard_map/ppermute | solution.py:111
  514.1 187.0 %collective-permute-start.7 = (f32[8,16,64,128]{3,2,1,0:T(8,128)}, f32[8,16,64,128]{3,2,1,0:T(8,128)}, u32[]{:S(2)}, u32[]{:S(2)}) collective-permute-start(f32[8,16,64,128]{3,2,1,0:T(8,128)} %multiply_add_fusion.1), channel_id=1, source_target_pairs={{0,8},{1,9},{2,10},{3,11},{4,12},{5,13},{6,14},{7,15},{16,24},{17,... | collective-permute-start | bytes 12582920 | tf_op jit(solution)/shard_map/ppermute | solution.py:112
  612.9 88.1 %collective-permute-start.3 = (f32[8,16]{1,0:T(8,128)S(1)}, f32[8,16]{1,0:T(8,128)S(1)}, u32[]{:S(2)}, u32[]{:S(2)}) collective-permute-start(f32[8,16]{1,0:T(8,128)S(1)} %select_multiply_fusion.1), channel_id=1, source_target_pairs={{0,4},{1,5},{2,6},{3,7},{4,8},{5,9},{6,10},{7,11},{8,12},{9,13},{1... | collective-permute-start | bytes 1544 | tf_op jit(solution)/shard_map/ppermute | solution.py:111
  701.0 108.6 %copy-start.16 = (f32[128]{0:T(128)S(1)}, f32[128]{0:T(128)}, u32[]{:S(2)}) copy-start(f32[128]{0:T(128)} %param.17) | copy-start | bytes 1540
  701.0 112.0 %copy-start.2 = (f32[2,256,8,16]{3,2,1,0:T(8,128)S(1)}, f32[2,256,8,16]{3,2,1,0:T(8,128)}, u32[]{:S(2)}) copy-start(f32[2,256,8,16]{3,2,1,0:T(8,128)} %get-tuple-element.16) | copy-start | bytes 786436
  707.1 169.8 %collective-permute-start.8 = (f32[8,16,64,128]{3,2,1,0:T(8,128)}, f32[8,16,64,128]{3,2,1,0:T(8,128)}, u32[]{:S(2)}, u32[]{:S(2)}) collective-permute-start(f32[8,16,64,128]{3,2,1,0:T(8,128)} %multiply_add_fusion), channel_id=1, source_target_pairs={{0,1},{1,2},{2,3},{3,4},{4,5},{5,6},{6,7},{7,8},{8,9},{9,10},{10,1... | collective-permute-start | bytes 12582920 | tf_op jit(solution)/shard_map/ppermute | solution.py:116
  813.7 17.6 %copy-start.10 = (f32[8,1024]{1,0:T(8,128)S(1)}, f32[8,1024]{1,0:T(8,128)}, u32[]{:S(2)}) copy-start(f32[8,1024]{1,0:T(8,128)} %param.18) | copy-start | bytes 98308
  813.7 19.0 %copy-start.4 = (bf16[64,8,8,128]{3,1,2,0:T(8,128)(2,1)S(1)}, bf16[64,8,8,128]{3,1,2,0:T(8,128)(2,1)}, u32[]{:S(2)}) copy-start(bf16[64,8,8,128]{3,1,2,0:T(8,128)(2,1)} %get-tuple-element.11) | copy-start | bytes 3145732
  851.3 25.7 %copy-start.7 = (f32[2,8,16]{2,1,0:T(8,128)S(1)}, f32[2,8,16]{2,1,0:T(8,128)}, u32[]{:S(2)}) copy-start(f32[2,8,16]{2,1,0:T(8,128)} %copy-done.6) | copy-start | bytes 3076
  1011.1 27.9 %copy-start.9 = (f32[8192]{0:T(1024)S(1)}, f32[8192]{0:T(1024)}, u32[]{:S(2)}) copy-start(f32[8192]{0:T(1024)} %mul.340) | copy-start | bytes 98308
  1011.1 27.9 %copy-start.11 = (f32[1,8,8,128]{3,1,2,0:T(8,128)S(1)}, f32[1,8,8,128]{3,1,2,0:T(8,128)}, u32[]{:S(2)}) copy-start(f32[1,8,8,128]{3,1,2,0:T(8,128)} %copy.188) | copy-start | bytes 98308
where the time goes:
time: 1100 us; the launch traced here: 1090 us
  waiting for transfers between devices  300 us (27%)
  matrix products  228 us (21%)
  starting transfers between devices  222 us (20%)
  local copies, waits for them, and re-layouts  217 us (20%)
  other arithmetic  125 us (11%)
    ppermute x3, waiting for transfers between devices, layer_shard(): got_decay = lax.ppermute(acc_decay, 'sp', hop_pairs)  255 us
    ppermute x4, starting transfers between devices, layer_shard(): got_state = lax.ppermute(acc_state, 'sp', hop_pairs)  116 us
    dot_general x1, matrix products, layer_shard(): jnp.dot(x, w_in, preferred_element_type=jnp.float32).astype(jnp.bfloat16)  92.6 us
    ppermute x1, starting transfers between devices, layer_shard(): state_in = lax.ppermute(acc_state, 'sp', next_pairs)  91.5 us
    reshape x3, local copies, waits for them, and re-layouts, finish_layer(): (y_intra + y_state).reshape(n_tok, n_heads, head_dim)  80 us
    dot_general x1, matrix products, finish_layer(): jnp.dot(normed.reshape(n_tok, d_inner).astype(jnp.bfloat16), w_out, prefe...  53.4 us
    ppermute x4, waiting for transfers between devices, layer_shard(): got_state = lax.ppermute(acc_state, 'sp', hop_pairs)  45.4 us
    dot_general x1, matrix products, local_scan(): jnp.einsum('cdgk,dgkpn->cgkpn', carry_w, chunk_state, precision=lax.Preci...  32 us
  transfers between devices with their start and end apart: 9, of which 4 were waited for; matrix products, arithmetic and copies ran while one was open for 11% of the time, Pallas kernels for 0%

commit v1 on v0

v1 whole, which is shorter than its diff:
```python
import functools
import jax
import jax.numpy as jnp
from jax import lax
from jax.experimental import pallas as pl
from jax.experimental.pallas import tpu as pltpu
from jax.sharding import PartitionSpec as P

CHUNK = 256
EPS = 1e-5
LOG2E = 1.4426950408889634
HALO = 16
COLS = 256
LAG = 3
VMEM = pltpu.VMEM
MESH = pl.DeviceIdType.MESH
F32 = jnp.float32
BF16 = jnp.bfloat16


def split3(v):
    hi = v.astype(BF16)
    rest = v - hi.astype(F32)
    mid = rest.astype(BF16)
    lo = (rest - mid.astype(F32)).astype(BF16)
    return hi, mid, lo


def dot(a, b):
    return jnp.dot(a, b, preferred_element_type=F32)


def dot_nt(a, b):
    return lax.dot_general(a, b, (((1,), (1,)), ((), ())), preferred_element_type=F32)


def prep_kernel(per, x_ref, w_ref, bias_ref, alog_ref, docc_ref, docr_ref, e_ref,
                aig_ref, ajt_ref, wst_ref, wend_ref, eexp_ref, dall_ref, mask_ref,
                tail_ref, segc_ref, segr_ref, keep_ref):
    n_tok = x_ref.shape[0]
    groups = aig_ref.shape[0]
    n_chunks = n_tok // CHUNK
    raw = dot(x_ref[...], w_ref[...]).astype(BF16).astype(F32) + bias_ref[...]
    dt = jnp.maximum(raw, 0.0) + jnp.log1p(jnp.exp(-jnp.abs(raw)))
    a = -jnp.exp(alog_ref[...]) * dt
    row = lax.broadcasted_iota(jnp.int32, (CHUNK, CHUNK), 0)
    col = lax.broadcasted_iota(jnp.int32, (CHUNK, CHUNK), 1)
    tri = (row >= col).astype(F32).astype(BF16)
    last_rows = []
    for c in range(n_chunks):
        rows = pl.ds(c * CHUNK, CHUNK)
        sl = slice(c * CHUNK, (c + 1) * CHUNK)
        hi, mid, lo = split3(a[sl])
        acum = dot(tri, hi) + (dot(tri, mid) + dot(tri, lo))
        dtc = dt[sl]
        segc = dot(tri, docc_ref[rows, :])
        segc_ref[rows, :] = segc
        segr_ref[:, rows] = dot_nt(docr_ref[:, rows], tri)
        a_last = acum[CHUNK - 1:CHUNK]
        s_last = segc[CHUNK - 1:CHUNK]
        wend = jnp.where(segc == s_last, jnp.exp(a_last - acum) * dtc, 0.0)
        wst = jnp.where(segc == 0.0, jnp.exp(acum), 0.0)
        e_c = jnp.where(s_last == 0.0, jnp.exp(a_last), 0.0)
        last_rows.append(e_c)
        ai = acum * LOG2E
        ajt_ref[:, rows] = (ai - jnp.log2(dtc)).T
        end3 = split3(wend)
        st3 = split3(wst)
        for g in range(groups):
            lanes = slice(g * per, (g + 1) * per)
            aig_ref[g, rows, :] = ai[:, lanes]
            wend_ref[g, rows, :] = jnp.concatenate([v[:, lanes] for v in end3], axis=1)
            wst_ref[g, rows, :] = jnp.concatenate([v[:, lanes] for v in st3], axis=1)
    total = last_rows[0]
    for e_c in last_rows[1:]:
        total = total * e_c
    n_row = len(last_rows)
    stack = jnp.concatenate(last_rows + [total] * (8 - n_row), axis=0)
    parts = split3(stack)
    for g in range(groups):
        lanes = slice(g * per, (g + 1) * per)
        cat = jnp.concatenate([v[:, lanes] for v in parts], axis=1)
        ex = dot(cat, e_ref[...])
        eexp_ref[g] = ex
        dall_ref[pl.ds(g, 1), :] = ex[n_row:n_row + 1]
    docf = docc_ref[...].astype(F32)
    keep_ref[pl.ds(0, 8), :] = jnp.ones((8, docf.shape[1]), F32)
    keep_ref[pl.ds(8, n_tok), :] = 1.0 - docf
    m1 = keep_ref[pl.ds(8, n_tok), :]
    m2 = m1 * keep_ref[pl.ds(7, n_tok), :]
    m3 = m2 * keep_ref[pl.ds(6, n_tok), :]
    mask_ref[0] = m1
    mask_ref[1] = m2
    mask_ref[2] = m3
    r16 = lax.broadcasted_iota(jnp.int32, (HALO, HALO), 0)
    c16 = lax.broadcasted_iota(jnp.int32, (HALO, HALO), 1)
    later = (c16 > r16).astype(F32).astype(BF16)
    cnt = dot(later, docc_ref[pl.ds(n_tok - HALO, HALO), :])
    tail = x_ref[pl.ds(n_tok - HALO, HALO), :].astype(F32)
    tail_ref[...] = jnp.where(cnt[:, :1] == 0.0, tail, 0.0).astype(BF16)


def proj_kernel(n_seq, groups, x_hbm, tail_ref, wa_ref, wbc_ref, cwx_ref, cwb_ref,
                mask_ref, wend_ref, eexp_ref, dall_ref, e_ref,
                xo_ref, bco_ref, z_ref, st0_ref, sin_hbm,
                xext, pbuf, btbuf, sloc, s1buf, rbuf, dpart,
                send_a, send_b, recv_s, recv_r, out_sem, misc):
    j = pl.program_id(0)
    idx = lax.axis_index('sp')
    core = lax.rem(idx, 2)
    chip = lax.div(idx, 2)
    n_chip = n_seq // 2
    n_tok = x_hbm.shape[0]
    n_chunks = n_tok // CHUNK
    n_q = wa_ref.shape[1] // COLS
    pieces = sloc.shape[0]
    halo_rows = pl.ds(0, HALO)

    def tail_copy(target):
        return pltpu.make_async_remote_copy(
            src_ref=tail_ref, dst_ref=xext.at[halo_rows], send_sem=misc.at[1], recv_sem=misc.at[2],
            device_id={'sp': target}, device_id_type=MESH)

    def decay_copy(target):
        return pltpu.make_async_remote_copy(
            src_ref=dall_ref, dst_ref=dpart, send_sem=misc.at[3], recv_sem=misc.at[4],
            device_id={'sp': target}, device_id_type=MESH)

    def state_copy(p, target):
        return pltpu.make_async_remote_copy(
            src_ref=sloc.at[p], dst_ref=s1buf.at[p], send_sem=send_a.at[p], recv_sem=recv_s.at[p],
            device_id={'sp': target}, device_id_type=MESH)

    def entry_copy(p, target):
        return pltpu.make_async_remote_copy(
            src_ref=sloc.at[p], dst_ref=rbuf.at[p], send_sem=send_a.at[p], recv_sem=recv_r.at[p],
            device_id={'sp': target}, device_id_type=MESH)

    def chain_copy(p, target):
        return pltpu.make_async_remote_copy(
            src_ref=s1buf.at[p], dst_ref=rbuf.at[p], send_sem=send_b.at[p], recv_sem=recv_r.at[p],
            device_id={'sp': target}, device_id_type=MESH)

    def out_copy(p):
        return pltpu.make_async_copy(rbuf.at[p], sin_hbm.at[p], out_sem.at[p])

    @pl.when(j == 0)
    def _():
        own = pltpu.make_async_copy(x_hbm, xext.at[pl.ds(HALO, n_tok)], misc.at[0])
        own.start()
        barrier = pltpu.get_barrier_semaphore()
        links = [(idx > 0, idx - 1), (idx < n_seq - 1, idx + 1),
                 ((core == 0) & (idx > 1), idx - 2), ((core == 0) & (idx < n_seq - 2), idx + 2)]
        for ok, other in links:
            @pl.when(ok)
            def _(other=other):
                pl.semaphore_signal(barrier, inc=1, device_id={'sp': other}, device_id_type=MESH)
        pl.semaphore_wait(barrier, sum(ok.astype(jnp.int32) for ok, other in links))

        @pl.when(idx < n_seq - 1)
        def _():
            tail_copy(idx + 1).start()

        @pl.when(core == 1)
        def _():
            decay_copy(idx - 1).start()

        @pl.when(idx == 0)
        def _():
            xext[halo_rows, :] = jnp.zeros((HALO, xext.shape[1]), BF16)

            def clear(p, carry):
                rbuf[p] = jnp.zeros(rbuf.shape[1:], F32)
                return carry
            lax.fori_loop(0, pieces, clear, 0)

        @pl.when(idx > 0)
        def _():
            tail_copy(idx).wait_recv()
        own.wait()

    def tick(t):
        @pl.when((core == 1) & (t < pieces))
        def _():
            state_copy(t, idx - 1).start()

        p = t - 1 - LAG * chip

        @pl.when((core == 0) & (p >= 0) & (p < pieces))
        def _():
            @pl.when(p == 0)
            def _():
                decay_copy(idx).wait_recv()
            state_copy(p, idx).wait_recv()

            @pl.when(chip > 0)
            def _():
                entry_copy(p, idx).wait_recv()
            grp = lax.div(p, n_q)
            lanes = pl.ds(pl.multiple_of(lax.rem(p, n_q) * COLS, COLS), COLS)
            d_own = dall_ref[pl.ds(grp, 1), lanes]
            d_par = dpart[pl.ds(grp, 1), lanes]
            mid = d_own * rbuf[p] + sloc[p]
            sloc[p] = mid
            s1buf[p] = d_par * mid + s1buf[p]

            @pl.when(chip < n_chip - 1)
            def _():
                chain_copy(p, idx + 2).start()
            entry_copy(p, idx + 1).start()
            out_copy(p).start()

        r = p - 2

        @pl.when((core == 1) & (r >= 0) & (r < pieces))
        def _():
            entry_copy(r, idx).wait_recv()
            out_copy(r).start()

    def conv(slot, cw_ref, lanes):
        buf = pbuf.at[slot]
        acc = cw_ref[4:5, lanes] + cw_ref[0:1, lanes] * buf[pl.ds(HALO, n_tok), :]
        for k in range(1, 4):
            m = mask_ref[k - 1]
            m = jnp.concatenate([m] * (COLS // m.shape[1]), axis=1)
            acc = acc + cw_ref[k:k + 1, lanes] * (m * buf[pl.ds(HALO - k, n_tok), :])
        half = 0.5 * acc
        return (half + half * jnp.tanh(half)).astype(BF16)

    def project(w, slot):
        pbuf[slot] = dot(xext[...], w).astype(BF16).astype(F32)

    @pl.when(j < groups)
    def _():
        par = lax.rem(j, 2)

        def epi_bc(slot):
            v = conv(slot, cwb_ref, slice(0, COLS))
            bco_ref[...] = v
            half = COLS // 2
            vt = v.T
            btbuf[2 * par] = vt[:half]
            btbuf[2 * par + 1] = vt[half:]

        def epi_x(q, slot):
            lanes = slice(q * COLS, (q + 1) * COLS)
            v = conv(slot, cwx_ref, lanes)
            xo_ref[:, lanes] = v
            wexp = dot(wend_ref[0], e_ref[:, lanes])
            xs = (v.astype(F32) * wexp).astype(BF16)
            tot = None
            for c in range(n_chunks):
                st = dot(btbuf[par, :, c * CHUNK:(c + 1) * CHUNK], xs[c * CHUNK:(c + 1) * CHUNK])
                if c == 0:
                    st0_ref[0, :, lanes] = st
                    tot = st
                else:
                    tot = eexp_ref[0, c:c + 1, lanes] * tot + st
            sloc[j * n_q + q] = tot

        project(wbc_ref[...], 0)
        for q in range(n_q):
            project(wa_ref[:, q * COLS:(q + 1) * COLS], (q + 1) % 2)
            if q == 0:
                epi_bc(0)
            else:
                epi_x(q - 1, q % 2)
                tick(j * n_q + q - 1)
        epi_x(n_q - 1, n_q % 2)
        tick(j * n_q + n_q - 1)

    @pl.when(j >= groups)
    def _():
        for q in range(n_q):
            lanes = slice(q * COLS, (q + 1) * COLS)
            z_ref[:, lanes] = dot(xext[pl.ds(HALO, n_tok), :], wa_ref[:, lanes]).astype(BF16)
            tick(j * n_q + q)

    @pl.when(j == 2 * groups - 1)
    def _():
        @pl.when(idx < n_seq - 1)
        def _():
            tail_copy(idx).wait_send()

        @pl.when(core == 1)
        def _():
            decay_copy(idx).wait_send()

        def drain(p, carry):
            state_copy(p, idx).wait_send()

            @pl.when((core == 0) & (chip < n_chip - 1))
            def _():
                chain_copy(p, idx).wait_send()
            out_copy(p).wait()
            return carry
        lax.fori_loop(0, pieces, drain, 0)


def mix_kernel(per, head, x_ref, z_ref, b_ref, c_ref, aig_ref, ajt_ref, wst_ref, segc_ref, segr_ref,
               sin_ref, st0_ref, eexp_ref, e_ref, skip_ref, norm_ref, o_ref, sc_ref, g_ref):
    n_tok, width = x_ref.shape
    n_chunks = n_tok // CHUNK
    half = CHUNK // 2
    pair = 2 * head
    row = lax.broadcasted_iota(jnp.int32, (CHUNK, CHUNK), 0)
    col = lax.broadcasted_iota(jnp.int32, (CHUNK, CHUNK), 1)
    first = lax.broadcasted_iota(jnp.int32, (half, pair), 1) < head
    n_piece = sin_ref.shape[0]
    pw = sin_ref.shape[2]
    for c in range(n_chunks):
        rows = slice(c * CHUNK, (c + 1) * CHUNK)
        cc = c_ref[rows, :]
        raw = dot_nt(cc, b_ref[rows, :])
        sc = segc_ref[rows, :]
        sc = jnp.concatenate([sc] * (CHUNK // sc.shape[1]), axis=1)
        same = sc == segr_ref[0:1, rows]
        sc_ref[...] = jnp.where(same & (row >= col), raw, 0.0)
        wst = wst_ref[0, rows, :]
        for k in range(n_piece):
            lanes = slice(k * pw, (k + 1) * pw)
            state = sin_ref[k]
            if c > 0:
                state = eexp_ref[0, 0:1, lanes] * state + st0_ref[0, :, lanes]
            ys = dot(cc, state.astype(BF16)) * dot(wst, e_ref[:, lanes])
            g_ref[:, lanes] = ys + skip_ref[0, :, lanes] * x_ref[rows, lanes].astype(F32)
        for hp in range(per // 2):
            lanes = slice(hp * pair, (hp + 1) * pair)
            xp = x_ref[rows, lanes]
            tops, bots = [], []
            for hh in range(2):
                h = 2 * hp + hh
                aj = ajt_ref[h:h + 1, rows]
                ai_t = aig_ref[0, c * CHUNK:c * CHUNK + half, h:h + 1]
                ai_b = aig_ref[0, c * CHUNK + half:(c + 1) * CHUNK, h:h + 1]
                m_tt = sc_ref[0:half, 0:half] * jnp.exp2(jnp.minimum(ai_t - aj[:, 0:half], 127.99))
                m_bl = sc_ref[half:CHUNK, 0:half] * jnp.exp2(jnp.minimum(ai_b - aj[:, 0:half], 127.99))
                m_br = sc_ref[half:CHUNK, half:CHUNK] * jnp.exp2(jnp.minimum(ai_b - aj[:, half:CHUNK], 127.99))
                tops.append(dot(m_tt.astype(BF16), xp[0:half]))
                m_b = jnp.concatenate([m_bl.astype(BF16), m_br.astype(BF16)], axis=1)
                bots.append(dot(m_b, xp))
            g_ref[0:half, lanes] += jnp.where(first, tops[0], tops[1])
            g_ref[half:CHUNK, lanes] += jnp.where(first, bots[0], bots[1])
        zf = z_ref[rows, :].astype(F32)
        hz = 0.5 * zf
        gated = g_ref[...] * (hz + hz * jnp.tanh(hz))
        mean = jnp.sum(gated * gated, axis=1, keepdims=True) * (1.0 / width)
        o_ref[rows, :] = (gated * lax.rsqrt(mean + EPS) * norm_ref[0]).astype(BF16)


def out_kernel(g_ref, w_ref, o_ref):
    o_ref[...] = dot(g_ref[...], w_ref[...]).astype(BF16)


def solution(mesh):
    n_seq = mesh.shape['sp']
    row_spec = P(('dp', 'sp'), None)
    tok_spec = P(('dp', 'sp'))

    def layer_shard(x, doc_start, w_in, conv_w, conv_b, dt_bias, a_log, d_skip, norm_w, w_out):
        n_tok, d_model = x.shape
        groups, gw = norm_w.shape
        d_inner = groups * gw
        n_heads = a_log.shape[0]
        per = n_heads // groups
        head = d_inner // n_heads
        conv_dim = conv_w.shape[1]
        sdim = (conv_dim - d_inner) // (2 * groups)
        n_q = gw // COLS
        pieces = groups * n_q
        lim = 67043328

        lane_head = jnp.arange(gw) // head
        expand = (lane_head[None, :] == jnp.arange(per)[:, None])
        expand = jnp.concatenate([expand] * 3, axis=0).astype(BF16)
        docf = doc_start.astype(BF16)
        docc = jnp.broadcast_to(docf[:, None], (n_tok, 128))
        docr = jnp.broadcast_to(docf[None, :], (8, n_tok))
        cw = jnp.concatenate([conv_w, conv_b[None], jnp.zeros((3, conv_dim), F32)], axis=0)
        skip = jnp.repeat(d_skip, head).reshape(groups, 1, gw)

        sds = jax.ShapeDtypeStruct
        full = lambda *shape: pl.BlockSpec(shape, lambda i: (0,) * len(shape))
        k3 = 3 * per
        dt_block = (d_inner + conv_dim) // n_heads
        prep = pl.pallas_call(
            functools.partial(prep_kernel, per),
            grid=(1,),
            in_specs=[full(n_tok, d_model), pl.BlockSpec((d_model, n_heads), lambda i: (0, dt_block)),
                      full(1, n_heads), full(1, n_heads), full(n_tok, 128), full(8, n_tok), full(k3, gw)],
            out_specs=[full(groups, n_tok, per), full(n_heads, n_tok), full(groups, n_tok, k3), full(groups, n_tok, k3),
                       full(groups, 8, gw), full(groups, gw), full(3, n_tok, 128), full(HALO, d_model),
                       full(n_tok, 128), full(8, n_tok)],
            out_shape=[sds((groups, n_tok, per), F32), sds((n_heads, n_tok), F32), sds((groups, n_tok, k3), BF16),
                       sds((groups, n_tok, k3), BF16), sds((groups, 8, gw), F32), sds((groups, gw), F32),
                       sds((3, n_tok, 128), F32), sds((HALO, d_model), BF16), sds((n_tok, 128), F32), sds((8, n_tok), F32)],
            scratch_shapes=[VMEM((n_tok + 8, 128), F32)],
            compiler_params=pltpu.CompilerParams(vmem_limit_bytes=lim),
            name='prep',
        )
        aig, ajt, wst3, wend3, eexp, dall, masks, tail, segc, segr = prep(
            x, w_in, dt_bias[None], a_log[None], docc, docr, expand)

        cap = lambda i: jnp.minimum(i, groups - 1)
        z_of = lambda i: jnp.maximum(i - groups, 0)
        pairs = groups // 2
        bc_of = lambda i: lax.rem(cap(i), 2) * pairs + lax.div(cap(i), 2)
        x_blk = d_inner // gw
        bc_blk = 2 * d_inner // COLS
        cb_blk = d_inner // COLS
        proj = pl.pallas_call(
            functools.partial(proj_kernel, n_seq, groups),
            grid=(2 * groups,),
            in_specs=[pl.BlockSpec(memory_space=pl.ANY), full(HALO, d_model),
                      pl.BlockSpec((d_model, gw), lambda i: (0, jnp.where(i < groups, i + x_blk, i - groups))),
                      pl.BlockSpec((d_model, COLS), lambda i: (0, bc_blk + bc_of(i))),
                      pl.BlockSpec((8, gw), lambda i: (0, cap(i))),
                      pl.BlockSpec((8, COLS), lambda i: (0, cb_blk + bc_of(i))),
                      full(3, n_tok, 128),
                      pl.BlockSpec((1, n_tok, k3), lambda i: (cap(i), 0, 0)),
                      pl.BlockSpec((1, 8, gw), lambda i: (cap(i), 0, 0)),
                      full(groups, gw), full(k3, gw)],
            out_specs=[pl.BlockSpec((n_tok, gw), lambda i: (0, cap(i))),
                       pl.BlockSpec((n_tok, COLS), lambda i: (0, bc_of(i))),
                       pl.BlockSpec((n_tok, gw), lambda i: (0, z_of(i))),
                       pl.BlockSpec((1, sdim, gw), lambda i: (cap(i), 0, 0)),
                       pl.BlockSpec(memory_space=pl.ANY)],
            out_shape=[sds((n_tok, d_inner), BF16), sds((n_tok, conv_dim - d_inner), BF16), sds((n_tok, d_inner), BF16),
                       sds((groups, sdim, gw), F32), sds((pieces, sdim, COLS), F32)],
            scratch_shapes=[VMEM((n_tok + HALO, d_model), BF16), VMEM((2, n_tok + HALO, COLS), F32),
                            VMEM((4, sdim, n_tok), BF16), VMEM((pieces, sdim, COLS), F32),
                            VMEM((pieces, sdim, COLS), F32), VMEM((pieces, sdim, COLS), F32), VMEM((groups, gw), F32),
                            pltpu.SemaphoreType.DMA((pieces,)), pltpu.SemaphoreType.DMA((pieces,)),
                            pltpu.SemaphoreType.DMA((pieces,)), pltpu.SemaphoreType.DMA((pieces,)),
                            pltpu.SemaphoreType.DMA((pieces,)), pltpu.SemaphoreType.DMA((5,))],
            compiler_params=pltpu.CompilerParams(vmem_limit_bytes=lim, collective_id=0, has_side_effects=True),
            name='proj',
        )
        xc, bc, z, st0, s_in = proj(x, tail, w_in, w_in, cw, cw, masks, wend3, eexp, dall, expand)

        mix = pl.pallas_call(
            functools.partial(mix_kernel, per, head),
            grid=(groups,),
            in_specs=[pl.BlockSpec((n_tok, gw), lambda i: (0, i)), pl.BlockSpec((n_tok, gw), lambda i: (0, i)),
                      pl.BlockSpec((n_tok, sdim), lambda i: (0, i)), pl.BlockSpec((n_tok, sdim), lambda i: (0, groups + i)),
                      pl.BlockSpec((1, n_tok, per), lambda i: (i, 0, 0)), pl.BlockSpec((per, n_tok), lambda i: (i, 0)),
                      pl.BlockSpec((1, n_tok, k3), lambda i: (i, 0, 0)), full(n_tok, 128), full(8, n_tok),
                      pl.BlockSpec((n_q, sdim, COLS), lambda i: (i, 0, 0)), pl.BlockSpec((1, sdim, gw), lambda i: (i, 0, 0)),
                      pl.BlockSpec((1, 8, gw), lambda i: (i, 0, 0)), full(k3, gw),
                      pl.BlockSpec((1, 1, gw), lambda i: (i, 0, 0)), pl.BlockSpec((1, 1, gw), lambda i: (i, 0, 0))],
            out_specs=pl.BlockSpec((n_tok, gw), lambda i: (0, i)),
            out_shape=sds((n_tok, d_inner), BF16),
            scratch_shapes=[VMEM((CHUNK, CHUNK), F32), VMEM((CHUNK, gw), F32)],
            compiler_params=pltpu.CompilerParams(vmem_limit_bytes=lim),
            name='mix',
        )
        g = mix(xc, z, bc, bc, aig, ajt, wst3, segc, segr, s_in, st0, eexp, expand, skip, norm_w[:, None, :])

        out_cols = 512
        out = pl.pallas_call(
            out_kernel,
            grid=(d_model // out_cols,),
            in_specs=[full(n_tok, d_inner), pl.BlockSpec((d_inner, out_cols), lambda i: (0, i))],
            out_specs=pl.BlockSpec((n_tok, out_cols), lambda i: (0, i)),
            out_shape=sds((n_tok, d_model), BF16),
            compiler_params=pltpu.CompilerParams(vmem_limit_bytes=lim),
            name='outproj',
        )
        return out(g, w_out)

    return jax.shard_map(layer_shard, mesh=mesh, in_specs=(row_spec, tok_spec, P(), P(), P(), P(), P(), P(), P(), P()), out_specs=row_spec, check_vma=False)
```

time: 1100 us -> 263 us (0.24)
  waiting for transfers between devices: 300 us -> 0 us
  Pallas kernels: 0 us -> 255 us
  matrix products: 228 us -> 0 us
  starting transfers between devices: 222 us -> 0 us
  local copies, waits for them, and re-layouts: 217 us -> 4.34 us
  other arithmetic: 125 us -> 3.09 us
    ppermute x9 -> x0, waiting for transfers between devices: 300 us -> none  [the longest x3 255 us: layer_shard(): got_decay = lax.ppermute(acc_decay, 'sp', hop_pairs)]
    pallas_call x0 -> x4, Pallas kernels: none -> 255 us  [the longest x1 175 us: layer_shard(): proj(x, tail, w_in, w_in, cw, cw, masks, wend3, eexp, dall, expand)]
    dot_general x7 -> x0, matrix products: 228 us -> none  [the longest x1 92.6 us: layer_shard(): jnp.dot(x, w_in, preferred_element_type=jnp.float32).astype(jnp.bfloat16)]
    ppermute x9 -> x0, starting transfers between devices: 222 us -> none  [the longest x4 116 us: layer_shard(): got_state = lax.ppermute(acc_state, 'sp', hop_pairs)]
    reshape x9 -> x0, local copies, waits for them, and re-layouts: 112 us -> none  [the longest x3 80 us: finish_layer(): (y_intra + y_state).reshape(n_tok, n_heads, head_dim)]
    convert_element_type x7 -> x2, other arithmetic: 44.4 us -> 1.33 us  [the longest x1 0.68 us: layer_shard(): docf = doc_start.astype(BF16)]
    add x1 -> x0, local copies, waits for them, and re-layouts: 28.6 us -> none  [finish_layer(): y_intra + y_state]
    add x5 -> x0, other arithmetic: 23.9 us -> none  [the longest x4 20.7 us: layer_shard(): acc_state = acc_decay[..., None, None] * got_state + acc_state]
  transfers between devices with their start and end apart: 9 -> 0, of which waited for: 4 -> 0; matrix products, arithmetic and copies ran while one was open for 11% -> 0% of each run, Pallas kernels for 0% -> 0%
where the time goes in v1:
time: 263 us; the launch traced here: 262 us
  Pallas kernels  255 us (97%)
  local copies, waits for them, and re-layouts  4.34 us (2%)
  other arithmetic  3.09 us (1%)
    pallas_call x1, Pallas kernels, layer_shard(): proj(x, tail, w_in, w_in, cw, cw, masks, wend3, eexp, dall, expand)  175 us
    pallas_call x1, Pallas kernels, layer_shard(): return out(g, w_out)  42.6 us
    pallas_call x1, Pallas kernels, layer_shard(): mix(xc, z, bc, bc, aig, ajt, wst3, segc, segr, s_in, st0, eexp, expand, s...  27.8 us
    pallas_call x1, Pallas kernels, layer_shard(): prep(x, w_in, dt_bias[None], a_log[None], docc, docr, expand)  9.19 us

profile of v1, /device:TPU:21, one launch (start us, length us, event | category | flops | bytes accessed | tf_op | source)
XLA Modules:
  0.0 262.5 jit_solution(17673438054285266674)
XLA Ops:
  0.0 0.1 pad.2.clone
  0.1 0.7 convert_element_type.6
  0.8 0.7 broadcast_in_dim.42
  1.5 0.6 broadcast_in_dim.39.docr_ref
  2.1 1.4 broadcast_in_dim.45.norm_ref
  3.5 0.1 broadcast_in_dim.43
  3.6 0.7 broadcast_in_dim.44.skip_ref
  4.3 0.6 add_convert_fusion.e_ref
  4.9 0.8 broadcast_in_dim.38.docc_ref
  5.7 1.7 maximum_maximum_fusion.cwx_ref.cwb_ref
  7.4 9.2 %prep.1 = (f32[8,512,16]{2,1,0:T(8,128)}, f32[128,512]{1,0:T(8,128)}, bf16[8,512,48]{2,1,0:T(8,128)(2,1)}, bf16[8,512,48]{2,1,0:T(8,128)(2,1)}, f32[8,8,1024]{2,...) custom-call(bf16[512,4096]{1,0:T(8,128)(2,1)} %x_hbm.1, ...), custom_call_target="tpu_custom_call" | custom-call | tf_op jit(solution)/shard_map/prep/pallas_call | solution.py:401
  16.6 175.4 %proj.1 = (bf16[512,8192]{1,0:T(8,128)(2,1)}, bf16[512,2048]{1,0:T(8,128)(2,1)}, bf16[512,8192]{1,0:T(8,128)(2,1)}, f32[8,128,1024]{2,1,0:T(8,128)}, f32[32,128,256]{2,1,0:T(8,128)}) custom-call(bf16[512,4096]{1,0:T(8,128)(2,1)} %x_hbm.1, bf16[16,4096]{1,0:T(8,128)(2,1)} %get-tuple-element.20.tail_ref, bf16[4096,18560]{1,0:T(8,128)(2,1)} %wbc_ref.1, ...), custom_call_target="tpu_custom_call" | custom-call | tf_op jit(solution)/shard_map/proj/pallas_call | solution.py:439
  192.1 27.8 %mix.1.g_ref = bf16[512,8192]{1,0:T(8,128)(2,1)} custom-call(bf16[512,8192]{1,0:T(8,128)(2,1)} %get-tuple-element.25.x_ref, bf16[512,8192]{1,0:T(8,128)(2,1)} %get-tuple-element.26.z_ref, bf16[512,2048]{1,0:T(8,128)(2,1)} %get-tuple-element.27.b_ref.c_ref, bf16[512,2048]{1,0:T(8,128)(2,1)} %get-tuple-element.27.b_ref.c_ref, ...), custom_call_target="tpu_custom_call" | custom-call | tf_op jit(solution)/shard_map/mix/pallas_call | solution.py:457
  219.9 42.6 %outproj.1 = bf16[512,4096]{1,0:T(8,128)(2,1)} custom-call(bf16[512,8192]{1,0:T(8,128)(2,1)} %mix.1.g_ref, bf16[8192,4096]{1,0:T(8,128)(2,1)} %w_ref.3), custom_call_target="tpu_custom_call" | custom-call | tf_op jit(solution)/shard_map/outproj/pallas_call | solution.py:469
  (3 shorter events, 0.0 us)

commit v2 on v1

v2 whole, which is shorter than its diff:
```python
import functools
import jax
import jax.numpy as jnp
from jax import lax
from jax.experimental import pallas as pl
from jax.experimental.pallas import tpu as pltpu
from jax.sharding import PartitionSpec as P

CHUNK = 256
EPS = 1e-5
LOG2E = 1.4426950408889634
HALO = 16
COLS = 256
LAG = 3
VMEM = pltpu.VMEM
MESH = pl.DeviceIdType.MESH
F32 = jnp.float32
BF16 = jnp.bfloat16


def split3(v):
    hi = v.astype(BF16)
    rest = v - hi.astype(F32)
    mid = rest.astype(BF16)
    lo = (rest - mid.astype(F32)).astype(BF16)
    return hi, mid, lo


def dot(a, b):
    return jnp.dot(a, b, preferred_element_type=F32)


def dot_nt(a, b):
    return lax.dot_general(a, b, (((1,), (1,)), ((), ())), preferred_element_type=F32)


def prep_kernel(per, head, x_ref, w_ref, bias_ref, alog_ref, skip_ref, doc_ref,
                ai_ref, ajt_ref, wst_ref, wend_ref, eexp_ref, dall_ref, mask_ref,
                tail_ref, segc_ref, segr_ref, e_ref, keep_ref):
    n_tok = x_ref.shape[0]
    doc = doc_ref[...].astype(F32)
    docr = jnp.broadcast_to(doc, (8, n_tok)).astype(BF16)
    docf = jnp.broadcast_to(doc, (128, n_tok)).T
    docc = docf.astype(BF16)
    e_row = lax.rem(lax.broadcasted_iota(jnp.int32, e_ref.shape, 0), per)
    e_col = lax.div(lax.broadcasted_iota(jnp.int32, e_ref.shape, 1), head)
    expand = (e_row == e_col).astype(F32).astype(BF16)
    e_ref[...] = expand
    groups = wst_ref.shape[0]
    n_chunks = n_tok // CHUNK
    raw = dot(x_ref[...], w_ref[...]).astype(BF16).astype(F32) + bias_ref[...]
    dt = jnp.maximum(raw, 0.0) + jnp.log1p(jnp.exp(-jnp.abs(raw)))
    a = -jnp.exp(alog_ref[...]) * dt
    row = lax.broadcasted_iota(jnp.int32, (CHUNK, CHUNK), 0)
    col = lax.broadcasted_iota(jnp.int32, (CHUNK, CHUNK), 1)
    tri = (row >= col).astype(F32).astype(BF16)
    last_rows = []
    for c in range(n_chunks):
        rows = pl.ds(c * CHUNK, CHUNK)
        sl = slice(c * CHUNK, (c + 1) * CHUNK)
        hi, mid, lo = split3(a[sl])
        acum = dot(tri, hi) + (dot(tri, mid) + dot(tri, lo))
        dtc = dt[sl]
        segc = dot(tri, docc[sl])
        segc_ref[rows, :] = segc
        segr_ref[:, rows] = dot_nt(docr[:, sl], tri)
        a_last = acum[CHUNK - 1:CHUNK]
        s_last = segc[CHUNK - 1:CHUNK]
        wend = jnp.where(segc == s_last, jnp.exp(a_last - acum) * dtc, 0.0)
        wst = jnp.where(segc == 0.0, jnp.exp(acum), 0.0)
        e_c = jnp.where(s_last == 0.0, jnp.exp(a_last), 0.0)
        last_rows.append(e_c)
        ai = acum * LOG2E
        ai_ref[rows, :] = ai
        ajt_ref[:, rows] = (ai - jnp.log2(dtc)).T
        end3 = split3(wend)
        st3 = split3(wst)
        for g in range(groups):
            lanes = slice(g * per, (g + 1) * per)
            wend_ref[g, rows, :] = jnp.concatenate([v[:, lanes] for v in end3], axis=1)
            wst_ref[g, rows, :] = jnp.concatenate([v[:, lanes] for v in st3], axis=1)
    total = last_rows[0]
    for e_c in last_rows[1:]:
        total = total * e_c
    n_row = len(last_rows)
    stack = jnp.concatenate(last_rows + [total] * (7 - n_row) + [skip_ref[...]], axis=0)
    parts = split3(stack)
    for g in range(groups):
        lanes = slice(g * per, (g + 1) * per)
        cat = jnp.concatenate([v[:, lanes] for v in parts], axis=1)
        ex = dot(cat, expand)
        eexp_ref[g] = ex
        dall_ref[pl.ds(g, 1), :] = ex[n_row:n_row + 1]
    keep_ref[pl.ds(0, 8), :] = jnp.ones((8, docf.shape[1]), F32)
    keep_ref[pl.ds(8, n_tok), :] = 1.0 - docf
    m1 = keep_ref[pl.ds(8, n_tok), :]
    m2 = m1 * keep_ref[pl.ds(7, n_tok), :]
    m3 = m2 * keep_ref[pl.ds(6, n_tok), :]
    mask_ref[0] = m1
    mask_ref[1] = m2
    mask_ref[2] = m3
    r16 = lax.broadcasted_iota(jnp.int32, (HALO, HALO), 0)
    c16 = lax.broadcasted_iota(jnp.int32, (HALO, HALO), 1)
    later = (c16 > r16).astype(F32).astype(BF16)
    cnt = dot(later, docc[n_tok - HALO:])
    tail = x_ref[pl.ds(n_tok - HALO, HALO), :].astype(F32)
    tail_ref[...] = jnp.where(cnt[:, :1] == 0.0, tail, 0.0).astype(BF16)


def proj_kernel(n_seq, groups, x_hbm, tail_ref, wa_ref, wbc_ref, cwx_ref, cbx_ref, cwb_ref, cbb_ref,
                mask_ref, wend_ref, eexp_ref, dall_ref, e_ref,
                xo_ref, bco_ref, z_ref, st0_ref, sin_hbm,
                xext, pbuf, btbuf, sloc, s1buf, rbuf, dpart,
                send_a, send_b, recv_s, recv_r, out_sem, misc):
    j = pl.program_id(0)
    idx = lax.axis_index('sp')
    core = lax.rem(idx, 2)
    chip = lax.div(idx, 2)
    n_chip = n_seq // 2
    n_tok = x_hbm.shape[0]
    n_chunks = n_tok // CHUNK
    n_q = wa_ref.shape[1] // COLS
    pieces = sloc.shape[0]
    halo_rows = pl.ds(0, HALO)

    def tail_copy(target):
        return pltpu.make_async_remote_copy(
            src_ref=tail_ref, dst_ref=xext.at[halo_rows], send_sem=misc.at[1], recv_sem=misc.at[2],
            device_id={'sp': target}, device_id_type=MESH)

    def decay_copy(target):
        return pltpu.make_async_remote_copy(
            src_ref=dall_ref, dst_ref=dpart, send_sem=misc.at[3], recv_sem=misc.at[4],
            device_id={'sp': target}, device_id_type=MESH)

    def state_copy(p, target):
        return pltpu.make_async_remote_copy(
            src_ref=sloc.at[p], dst_ref=s1buf.at[p], send_sem=send_a.at[p], recv_sem=recv_s.at[p],
            device_id={'sp': target}, device_id_type=MESH)

    def entry_copy(p, target):
        return pltpu.make_async_remote_copy(
            src_ref=sloc.at[p], dst_ref=rbuf.at[p], send_sem=send_a.at[p], recv_sem=recv_r.at[p],
            device_id={'sp': target}, device_id_type=MESH)

    def chain_copy(p, target):
        return pltpu.make_async_remote_copy(
            src_ref=s1buf.at[p], dst_ref=rbuf.at[p], send_sem=send_b.at[p], recv_sem=recv_r.at[p],
            device_id={'sp': target}, device_id_type=MESH)

    def out_copy(p):
        return pltpu.make_async_copy(rbuf.at[p], sin_hbm.at[p], out_sem.at[p])

    @pl.when(j == 0)
    def _():
        own = pltpu.make_async_copy(x_hbm, xext.at[pl.ds(HALO, n_tok)], misc.at[0])
        own.start()
        barrier = pltpu.get_barrier_semaphore()
        links = [(idx > 0, idx - 1), (idx < n_seq - 1, idx + 1),
                 ((core == 0) & (idx > 1), idx - 2), ((core == 0) & (idx < n_seq - 2), idx + 2)]
        for ok, other in links:
            @pl.when(ok)
            def _(other=other):
                pl.semaphore_signal(barrier, inc=1, device_id={'sp': other}, device_id_type=MESH)
        pl.semaphore_wait(barrier, sum(ok.astype(jnp.int32) for ok, other in links))

        @pl.when(idx < n_seq - 1)
        def _():
            tail_copy(idx + 1).start()

        @pl.when(core == 1)
        def _():
            decay_copy(idx - 1).start()

        @pl.when(idx == 0)
        def _():
            xext[halo_rows, :] = jnp.zeros((HALO, xext.shape[1]), BF16)

            def clear(p, carry):
                rbuf[p] = jnp.zeros(rbuf.shape[1:], F32)
                return carry
            lax.fori_loop(0, pieces, clear, 0)

        @pl.when(idx > 0)
        def _():
            tail_copy(idx).wait_recv()
        own.wait()

    def tick(t):
        @pl.when((core == 1) & (t < pieces))
        def _():
            state_copy(t, idx - 1).start()

        p = t - 1 - LAG * chip

        @pl.when((core == 0) & (p >= 0) & (p < pieces))
        def _():
            @pl.when(p == 0)
            def _():
                decay_copy(idx).wait_recv()
            state_copy(p, idx).wait_recv()

            @pl.when(chip > 0)
            def _():
                entry_copy(p, idx).wait_recv()
            grp = lax.div(p, n_q)
            lanes = pl.ds(pl.multiple_of(lax.rem(p, n_q) * COLS, COLS), COLS)
            d_own = dall_ref[pl.ds(grp, 1), lanes]
            d_par = dpart[pl.ds(grp, 1), lanes]
            mid = d_own * rbuf[p] + sloc[p]
            sloc[p] = mid
            s1buf[p] = d_par * mid + s1buf[p]

            @pl.when(chip < n_chip - 1)
            def _():
                chain_copy(p, idx + 2).start()
            entry_copy(p, idx + 1).start()
            out_copy(p).start()

        r = p - 2

        @pl.when((core == 1) & (r >= 0) & (r < pieces))
        def _():
            entry_copy(r, idx).wait_recv()
            out_copy(r).start()

    def conv(cw_ref, cb_ref, lanes):
        acc = cb_ref[0:1, lanes] + cw_ref[0:1, lanes] * pbuf[pl.ds(HALO, n_tok), :]
        for k in range(1, 4):
            m = mask_ref[k - 1]
            m = jnp.concatenate([m] * (COLS // m.shape[1]), axis=1)
            acc = acc + cw_ref[k:k + 1, lanes] * (m * pbuf[pl.ds(HALO - k, n_tok), :])
        half = 0.5 * acc
        return (half + half * jnp.tanh(half)).astype(BF16)

    def project(w):
        pbuf[...] = dot(xext[...], w).astype(BF16).astype(F32)

    def lane_block(q):
        return pl.ds(pl.multiple_of(q * COLS, COLS), COLS)

    @pl.when(j < groups)
    def _():
        par = lax.rem(j, 2)

        def epi_bc():
            v = conv(cwb_ref, cbb_ref, slice(0, COLS))
            bco_ref[...] = v
            half = COLS // 2
            vt = v.T
            btbuf[2 * par] = vt[:half]
            btbuf[2 * par + 1] = vt[half:]

        def epi_x(q):
            lanes = lane_block(q)
            v = conv(cwx_ref, cbx_ref, lanes)
            xo_ref[:, lanes] = v
            wexp = dot(wend_ref[0], e_ref[:, lanes])
            xs = (v.astype(F32) * wexp).astype(BF16)
            tot = None
            for c in range(n_chunks):
                st = dot(btbuf[par, :, c * CHUNK:(c + 1) * CHUNK], xs[c * CHUNK:(c + 1) * CHUNK])
                if c == 0:
                    st0_ref[0, :, lanes] = st
                    tot = st
                else:
                    tot = eexp_ref[0, c:c + 1, lanes] * tot + st
            sloc[j * n_q + q] = tot

        project(wbc_ref[...])
        epi_bc()
        project(wa_ref[:, 0:COLS])

        def body(q, carry):
            epi_x(q)
            project(wa_ref[:, lane_block(q + 1)])
            tick(j * n_q + q)
            return carry
        lax.fori_loop(0, n_q - 1, body, 0)
        epi_x(n_q - 1)
        tick(j * n_q + n_q - 1)

    @pl.when(j >= groups)
    def _():
        def body(q, carry):
            lanes = lane_block(q)
            z_ref[:, lanes] = dot(xext[pl.ds(HALO, n_tok), :], wa_ref[:, lanes]).astype(BF16)
            tick(j * n_q + q)
            return carry
        lax.fori_loop(0, n_q, body, 0)

    @pl.when(j == 2 * groups - 1)
    def _():
        @pl.when(idx < n_seq - 1)
        def _():
            tail_copy(idx).wait_send()

        @pl.when(core == 1)
        def _():
            decay_copy(idx).wait_send()

        def drain(p, carry):
            state_copy(p, idx).wait_send()

            @pl.when((core == 0) & (chip < n_chip - 1))
            def _():
                chain_copy(p, idx).wait_send()
            out_copy(p).wait()
            return carry
        lax.fori_loop(0, pieces, drain, 0)


def finish_kernel(per, head, x_ref, z_ref, b_ref, c_ref, ai_ref, ajt_ref, wst_ref, segc_ref, segr_ref,
                  sin_ref, st0_ref, eexp_ref, e_ref, norm_ref, w_ref, o_ref, sc_ref, y_ref, g_ref, acc_ref):
    i = pl.program_id(0)
    groups = norm_ref.shape[0]
    n_tok, width = x_ref.shape
    n_heads = ai_ref.shape[1]
    n_chunks = n_tok // CHUNK
    half = CHUNK // 2
    pair = 2 * head
    n_q = width // COLS
    out_cols = w_ref.shape[1] // n_q

    def masked_scores():
        row = lax.broadcasted_iota(jnp.int32, (CHUNK, CHUNK), 0)
        col = lax.broadcasted_iota(jnp.int32, (CHUNK, CHUNK), 1)
        for c in range(n_chunks):
            rows = slice(c * CHUNK, (c + 1) * CHUNK)
            raw = dot_nt(c_ref[rows, :], b_ref[rows, :])
            sc = segc_ref[rows, :]
            sc = jnp.concatenate([sc] * (CHUNK // sc.shape[1]), axis=1)
            same = sc == segr_ref[0:1, rows]
            sc_ref[c] = jnp.where(same & (row >= col), raw, 0.0)

    def mix_quad(q):
        first = lax.broadcasted_iota(jnp.int32, (half, pair), 1) < head
        lanes = pl.ds(pl.multiple_of(q * COLS, COLS), COLS)
        per_q = COLS // head
        ai = pltpu.roll(ai_ref[...], lax.rem(n_heads - (i * per + q * per_q), n_heads), 1)
        for c in range(n_chunks):
            r0 = c * CHUNK
            rows = slice(r0, r0 + CHUNK)
            sc = sc_ref.at[c]
            state = sin_ref[q]
            if c > 0:
                state = eexp_ref[0, 0:1, lanes] * state + st0_ref[0, :, lanes]
            ys = dot(c_ref[rows, :], state.astype(BF16)) * dot(wst_ref[0, rows, :], e_ref[:, lanes])
            y_ref[rows, lanes] = ys + eexp_ref[0, 7:8, lanes] * x_ref[rows, lanes].astype(F32)
            for hp in range(per_q // 2):
                pl_lanes = pl.ds(pl.multiple_of(q * COLS + hp * pair, pair), pair)
                xp = x_ref[rows, pl_lanes]
                tops, bots = [], []
                for hh in range(2):
                    k = 2 * hp + hh
                    aj = ajt_ref[pl.ds(q * per_q + k, 1), rows]
                    ai_t = ai[r0:r0 + half, k:k + 1]
                    ai_b = ai[r0 + half:r0 + CHUNK, k:k + 1]
                    m_tt = sc[0:half, 0:half] * jnp.exp2(jnp.minimum(ai_t - aj[:, 0:half], 127.99))
                    m_bl = sc[half:CHUNK, 0:half] * jnp.exp2(jnp.minimum(ai_b - aj[:, 0:half], 127.99))
                    m_br = sc[half:CHUNK, half:CHUNK] * jnp.exp2(jnp.minimum(ai_b - aj[:, half:CHUNK], 127.99))
                    tops.append(dot(m_tt.astype(BF16), xp[0:half]))
                    m_b = jnp.concatenate([m_bl.astype(BF16), m_br.astype(BF16)], axis=1)
                    bots.append(dot(m_b, xp))
                for top, parts in ((r0, tops), (r0 + half, bots)):
                    sub = slice(top, top + half)
                    y = y_ref[sub, pl_lanes] + jnp.where(first, parts[0], parts[1])
                    hz = 0.5 * z_ref[sub, pl_lanes].astype(F32)
                    y_ref[sub, pl_lanes] = y * (hz + hz * jnp.tanh(hz))

    def normalize():
        y = y_ref[...]
        mean = jnp.sum(y * y, axis=1, keepdims=True) * (1.0 / width)
        g_ref[...] = (y * lax.rsqrt(mean + EPS) * norm_ref[pl.ds(i, 1), :]).astype(BF16)

    def out_part(q):
        cols = pl.ds(pl.multiple_of(q * out_cols, out_cols), out_cols)
        acc_ref[:, cols] += dot(g_ref[...], w_ref[:, cols])

    @pl.when(i == 0)
    def _():
        masked_scores()

        def body(q, carry):
            cols = pl.ds(pl.multiple_of(q * out_cols, out_cols), out_cols)
            acc_ref[:, cols] = jnp.zeros((n_tok, out_cols), F32)
            mix_quad(q)
            return carry
        lax.fori_loop(0, n_q, body, 0)
        normalize()

    @pl.when((i > 0) & (i < groups))
    def _():
        masked_scores()

        def body(q, carry):
            out_part(q)
            mix_quad(q)
            return carry
        lax.fori_loop(0, n_q, body, 0)
        normalize()

    @pl.when(i == groups)
    def _():
        def body(q, carry):
            cols = pl.ds(pl.multiple_of(q * out_cols, out_cols), out_cols)
            o_ref[:, cols] = (acc_ref[:, cols] + dot(g_ref[...], w_ref[:, cols])).astype(BF16)
            return carry
        lax.fori_loop(0, n_q, body, 0)


def solution(mesh):
    n_seq = mesh.shape['sp']
    row_spec = P(('dp', 'sp'), None)
    tok_spec = P(('dp', 'sp'))

    def layer_shard(x, doc_start, w_in, conv_w, conv_b, dt_bias, a_log, d_skip, norm_w, w_out):
        n_tok, d_model = x.shape
        groups, gw = norm_w.shape
        d_inner = groups * gw
        n_heads = a_log.shape[0]
        per = n_heads // groups
        head = d_inner // n_heads
        conv_dim = conv_w.shape[1]
        sdim = (conv_dim - d_inner) // (2 * groups)
        n_q = gw // COLS
        n_chunks = n_tok // CHUNK
        pieces = groups * n_q
        lim = 67043328

        sds = jax.ShapeDtypeStruct
        full = lambda *shape: pl.BlockSpec(shape, lambda i: (0,) * len(shape))
        k3 = 3 * per
        dt_block = (d_inner + conv_dim) // n_heads
        prep = pl.pallas_call(
            functools.partial(prep_kernel, per, head),
            grid=(1,),
            in_specs=[full(n_tok, d_model), pl.BlockSpec((d_model, n_heads), lambda i: (0, dt_block)),
                      full(1, n_heads), full(1, n_heads), full(1, n_heads), full(1, n_tok)],
            out_specs=[full(n_tok, n_heads), full(n_heads, n_tok), full(groups, n_tok, k3), full(groups, n_tok, k3),
                       full(groups, 8, gw), full(groups, gw), full(3, n_tok, 128), full(HALO, d_model),
                       full(n_tok, 128), full(8, n_tok), full(k3, gw)],
            out_shape=[sds((n_tok, n_heads), F32), sds((n_heads, n_tok), F32), sds((groups, n_tok, k3), BF16),
                       sds((groups, n_tok, k3), BF16), sds((groups, 8, gw), F32), sds((groups, gw), F32),
                       sds((3, n_tok, 128), F32), sds((HALO, d_model), BF16), sds((n_tok, 128), F32), sds((8, n_tok), F32), sds((k3, gw), BF16)],
            scratch_shapes=[VMEM((n_tok + 8, 128), F32)],
            compiler_params=pltpu.CompilerParams(vmem_limit_bytes=lim),
            name='prep',
        )
        ai, ajt, wst3, wend3, eexp, dall, masks, tail, segc, segr, expand = prep(
            x, w_in, dt_bias[None], a_log[None], d_skip[None], doc_start[None])

        cap = lambda i: jnp.minimum(i, groups - 1)
        z_of = lambda i: jnp.maximum(i - groups, 0)
        pairs = groups // 2
        bc_of = lambda i: lax.rem(cap(i), 2) * pairs + lax.div(cap(i), 2)
        x_blk = d_inner // gw
        bc_blk = 2 * d_inner // COLS
        cb_blk = d_inner // COLS
        proj = pl.pallas_call(
            functools.partial(proj_kernel, n_seq, groups),
            grid=(2 * groups,),
            in_specs=[pl.BlockSpec(memory_space=pl.ANY), full(HALO, d_model),
                      pl.BlockSpec((d_model, gw), lambda i: (0, jnp.where(i < groups, i + x_blk, i - groups))),
                      pl.BlockSpec((d_model, COLS), lambda i: (0, bc_blk + bc_of(i))),
                      pl.BlockSpec((4, gw), lambda i: (0, cap(i))), pl.BlockSpec((1, gw), lambda i: (0, cap(i))),
                      pl.BlockSpec((4, COLS), lambda i: (0, cb_blk + bc_of(i))), pl.BlockSpec((1, COLS), lambda i: (0, cb_blk + bc_of(i))),
                      full(3, n_tok, 128),
                      pl.BlockSpec((1, n_tok, k3), lambda i: (cap(i), 0, 0)),
                      pl.BlockSpec((1, 8, gw), lambda i: (cap(i), 0, 0)),
                      full(groups, gw), full(k3, gw)],
            out_specs=[pl.BlockSpec((n_tok, gw), lambda i: (0, cap(i))),
                       pl.BlockSpec((n_tok, COLS), lambda i: (0, bc_of(i))),
                       pl.BlockSpec((n_tok, gw), lambda i: (0, z_of(i))),
                       pl.BlockSpec((1, sdim, gw), lambda i: (cap(i), 0, 0)),
                       pl.BlockSpec(memory_space=pl.ANY)],
            out_shape=[sds((n_tok, d_inner), BF16), sds((n_tok, conv_dim - d_inner), BF16), sds((n_tok, d_inner), BF16),
                       sds((groups, sdim, gw), F32), sds((pieces, sdim, COLS), F32)],
            scratch_shapes=[VMEM((n_tok + HALO, d_model), BF16), VMEM((n_tok + HALO, COLS), F32),
                            VMEM((4, sdim, n_tok), BF16), VMEM((pieces, sdim, COLS), F32),
                            VMEM((pieces, sdim, COLS), F32), VMEM((pieces, sdim, COLS), F32), VMEM((groups, gw), F32),
                            pltpu.SemaphoreType.DMA((pieces,)), pltpu.SemaphoreType.DMA((pieces,)),
                            pltpu.SemaphoreType.DMA((pieces,)), pltpu.SemaphoreType.DMA((pieces,)),
                            pltpu.SemaphoreType.DMA((pieces,)), pltpu.SemaphoreType.DMA((5,))],
            compiler_params=pltpu.CompilerParams(vmem_limit_bytes=lim, collective_id=0, has_side_effects=True),
            name='proj',
        )
        xc, bc, z, st0, s_in = proj(x, tail, w_in, w_in, conv_w, conv_b[None], conv_w, conv_b[None], masks, wend3, eexp, dall, expand)

        prev = lambda i: jnp.maximum(i - 1, 0)
        finish = pl.pallas_call(
            functools.partial(finish_kernel, per, head),
            grid=(groups + 1,),
            in_specs=[pl.BlockSpec((n_tok, gw), lambda i: (0, cap(i))), pl.BlockSpec((n_tok, gw), lambda i: (0, cap(i))),
                      pl.BlockSpec((n_tok, sdim), lambda i: (0, cap(i))), pl.BlockSpec((n_tok, sdim), lambda i: (0, groups + cap(i))),
                      full(n_tok, n_heads), pl.BlockSpec((per, n_tok), lambda i: (cap(i), 0)),
                      pl.BlockSpec((1, n_tok, k3), lambda i: (cap(i), 0, 0)), full(n_tok, 128), full(8, n_tok),
                      pl.BlockSpec((n_q, sdim, COLS), lambda i: (cap(i), 0, 0)), pl.BlockSpec((1, sdim, gw), lambda i: (cap(i), 0, 0)),
                      pl.BlockSpec((1, 8, gw), lambda i: (cap(i), 0, 0)), full(k3, gw), full(groups, gw),
                      pl.BlockSpec((gw, d_model), lambda i: (prev(i), 0))],
            out_specs=full(n_tok, d_model),
            out_shape=sds((n_tok, d_model), BF16),
            scratch_shapes=[VMEM((n_chunks, CHUNK, CHUNK), F32), VMEM((n_tok, gw), F32), VMEM((n_tok, gw), BF16),
                            VMEM((n_tok, d_model), F32)],
            compiler_params=pltpu.CompilerParams(vmem_limit_bytes=lim),
            name='finish',
        )
        return finish(xc, z, bc, bc, ai, ajt, wst3, segc, segr, s_in, st0, eexp, expand, norm_w, w_out)

    return jax.shard_map(layer_shard, mesh=mesh, in_specs=(row_spec, tok_spec, P(), P(), P(), P(), P(), P(), P(), P()), out_specs=row_spec, check_vma=False)
```

time: 263 us -> 212 us (0.81)
  Pallas kernels: 255 us -> 212 us
  local copies, waits for them, and re-layouts: 4.34 us -> 0 us
  other arithmetic: 3.09 us -> 0 us
    pallas_call x4 -> x3, Pallas kernels: 255 us -> 212 us  [the longest x1 135 us: layer_shard(): proj(x, tail, w_in, w_in, conv_w, conv_b[None], conv_w, conv_b[None], mas...]
    broadcast_in_dim x7 -> x0, local copies, waits for them, and re-layouts: 4.27 us -> none  [the longest x3 1.51 us: layer_shard(): skip = jnp.repeat(d_skip, head).reshape(groups, 1, gw)]
where the time goes in v2:
time: 212 us
  Pallas kernels  212 us (100%)
    pallas_call x1, Pallas kernels, layer_shard(): proj(x, tail, w_in, w_in, conv_w, conv_b[None], conv_w, conv_b[None], mas...  135 us
    pallas_call x1, Pallas kernels, layer_shard(): finish(xc, z, bc, bc, ai, ajt, wst3, segc, segr, s_in, st0, eexp, expand,...  69.2 us
    pallas_call x1, Pallas kernels, layer_shard(): prep(x, w_in, dt_bias[None], a_log[None], d_skip[None], doc_start[None])  8.14 us

profile of v2, /device:TPU:21, one launch (start us, length us, event | category | flops | bytes accessed | tf_op | source)
XLA Modules:
  0.0 212.3 jit_solution(7773213659595816017)
XLA Ops:
  0.0 8.1 %prep.1 = (f32[512,128]{1,0:T(8,128)}, f32[128,512]{1,0:T(8,128)}, bf16[8,512,48]{2,1,0:T(8,128)(2,1)}, bf16[8,512,48]{2,1,0:T(8,128)(2,1)}, f32[8,8,1024]{2,1,0...) custom-call(bf16[512,4096]{1,0:T(8,128)(2,1)} %x_hbm.1, ...), custom_call_target="tpu_custom_call" | custom-call | tf_op jit(solution)/shard_map/prep/pallas_call | solution.py:450
  8.1 134.9 %proj.1 = (bf16[512,8192]{1,0:T(8,128)(2,1)}, bf16[512,2048]{1,0:T(8,128)(2,1)}, bf16[512,8192]{1,0:T(8,128)(2,1)}, f32[8,128,1024]{2,1,0:T(8,128)}, f32[32,128,256]{2,1,0:T(8,128)}) custom-call(bf16[512,4096]{1,0:T(8,128)(2,1)} %x_hbm.1, bf16[16,4096]{1,0:T(8,128)(2,1)} %get-tuple-element.21.tail_ref, bf16[4096,18560]{1,0:T(8,128)(2,1)} %wbc_ref.1, ...), custom_call_target="tpu_custom_call" | custom-call | tf_op jit(solution)/shard_map/proj/pallas_call | solution.py:488
  143.1 69.2 %finish.1 = bf16[512,4096]{1,0:T(8,128)(2,1)} custom-call(bf16[512,8192]{1,0:T(8,128)(2,1)} %get-tuple-element.27.x_ref, bf16[512,8192]{1,0:T(8,128)(2,1)} %get-tuple-element.28.z_ref, bf16[512,2048]{1,0:T(8,128)(2,1)} %get-tuple-element.29.b_ref.c_ref, bf16[512,2048]{1,0:T(8,128)(2,1)} %get-tuple-element.29.b_ref.c_ref, ...), custom_call_target="tpu_custom_call" | custom-call | tf_op jit(solution)/shard_map/finish/pallas_call | solution.py:508

commit v3 on v2

--- a/solution.py
+++ b/solution.py
@@ -10,8 +10,11 @@
 EPS = 1e-5
 LOG2E = 1.4426950408889634
 HALO = 16
-COLS = 256
-LAG = 3
+COLS = 512
+BC_COLS = 256
+QUAD = 512
+LAG = 2
+LAG_BACK = 1
 VMEM = pltpu.VMEM
 MESH = pl.DeviceIdType.MESH
 F32 = jnp.float32
@@ -110,7 +113,7 @@
 def proj_kernel(n_seq, groups, x_hbm, tail_ref, wa_ref, wbc_ref, cwx_ref, cbx_ref, cwb_ref, cbb_ref,
                 mask_ref, wend_ref, eexp_ref, dall_ref, e_ref,
                 xo_ref, bco_ref, z_ref, st0_ref, sin_hbm,
-                xext, pbuf, btbuf, sloc, s1buf, rbuf, dpart,
+                xext, pbuf, bbuf, btbuf, sloc, s1buf, rbuf, dpart,
                 send_a, send_b, recv_s, recv_r, out_sem, misc):
     j = pl.program_id(0)
     idx = lax.axis_index('sp')
@@ -217,43 +220,41 @@
             entry_copy(p, idx + 1).start()
             out_copy(p).start()
 
-        r = p - 2
+        r = p - LAG_BACK
 
         @pl.when((core == 1) & (r >= 0) & (r < pieces))
         def _():
             entry_copy(r, idx).wait_recv()
             out_copy(r).start()
 
-    def conv(cw_ref, cb_ref, lanes):
-        acc = cb_ref[0:1, lanes] + cw_ref[0:1, lanes] * pbuf[pl.ds(HALO, n_tok), :]
+    def conv(buf, cw_ref, cb_ref, lanes):
+        cols = buf.shape[1]
+        acc = cb_ref[0:1, lanes] + cw_ref[0:1, lanes] * buf[pl.ds(HALO, n_tok), :]
         for k in range(1, 4):
             m = mask_ref[k - 1]
-            m = jnp.concatenate([m] * (COLS // m.shape[1]), axis=1)
-            acc = acc + cw_ref[k:k + 1, lanes] * (m * pbuf[pl.ds(HALO - k, n_tok), :])
+            m = jnp.concatenate([m] * (cols // m.shape[1]), axis=1)
+            acc = acc + cw_ref[k:k + 1, lanes] * (m * buf[pl.ds(HALO - k, n_tok), :])
         half = 0.5 * acc
         return (half + half * jnp.tanh(half)).astype(BF16)
 
-    def project(w):
-        pbuf[...] = dot(xext[...], w).astype(BF16).astype(F32)
-
-    def lane_block(q):
-        return pl.ds(pl.multiple_of(q * COLS, COLS), COLS)
+    def project(buf, w):
+        buf[...] = dot(xext[...], w).astype(BF16).astype(F32)
 
     @pl.when(j < groups)
     def _():
         par = lax.rem(j, 2)
 
         def epi_bc():
-            v = conv(cwb_ref, cbb_ref, slice(0, COLS))
+            v = conv(bbuf, cwb_ref, cbb_ref, slice(0, BC_COLS))
             bco_ref[...] = v
-            half = COLS // 2
+            half = BC_COLS // 2
             vt = v.T
             btbuf[2 * par] = vt[:half]
             btbuf[2 * par + 1] = vt[half:]
 
-        def epi_x(q):
-            lanes = lane_block(q)
-            v = conv(cwx_ref, cbx_ref, lanes)
+        def epi_x(q, buf):
+            lanes = slice(q * COLS, (q + 1) * COLS)
+            v = conv(buf, cwx_ref, cbx_ref, lanes)
             xo_ref[:, lanes] = v
             wexp = dot(wend_ref[0], e_ref[:, lanes])
             xs = (v.astype(F32) * wexp).astype(BF16)
@@ -267,23 +268,20 @@
                     tot = eexp_ref[0, c:c + 1, lanes] * tot + st
             sloc[j * n_q + q] = tot
 
-        project(wbc_ref[...])
+        project(bbuf, wbc_ref[...])
+        project(pbuf.at[0], wa_ref[:, 0:COLS])
         epi_bc()
-        project(wa_ref[:, 0:COLS])
-
+        for q in range(n_q - 1):
+            project(pbuf.at[(q + 1) % 2], wa_ref[:, (q + 1) * COLS:(q + 2) * COLS])
+            epi_x(q, pbuf.at[q % 2])
+            tick(j * n_q + q)
+        epi_x(n_q - 1, pbuf.at[(n_q - 1) % 2])
+        tick(j * n_q + n_q - 1)
+
+    @pl.when(j >= groups)
+    def _():
         def body(q, carry):
-            epi_x(q)
-            project(wa_ref[:, lane_block(q + 1)])
-            tick(j * n_q + q)
-            return carry
-        lax.fori_loop(0, n_q - 1, body, 0)
-        epi_x(n_q - 1)
-        tick(j * n_q + n_q - 1)
-
-    @pl.when(j >= groups)
-    def _():
-        def body(q, carry):
-            lanes = lane_block(q)
+            lanes = pl.ds(pl.multiple_of(q * COLS, COLS), COLS)
             z_ref[:, lanes] = dot(xext[pl.ds(HALO, n_tok), :], wa_ref[:, lanes]).astype(BF16)
             tick(j * n_q + q)
             return carry
@@ -319,7 +317,8 @@
     n_chunks = n_tok // CHUNK
     half = CHUNK // 2
     pair = 2 * head
-    n_q = width // COLS
+    n_q = width // QUAD
+    n_sub = sin_ref.shape[2] // QUAD
     out_cols = w_ref.shape[1] // n_q
 
     def masked_scores():
@@ -335,20 +334,20 @@
 
     def mix_quad(q):
         first = lax.broadcasted_iota(jnp.int32, (half, pair), 1) < head
-        lanes = pl.ds(pl.multiple_of(q * COLS, COLS), COLS)
-        per_q = COLS // head
+        lanes = pl.ds(pl.multiple_of(q * QUAD, QUAD), QUAD)
+        per_q = QUAD // head
         ai = pltpu.roll(ai_ref[...], lax.rem(n_heads - (i * per + q * per_q), n_heads), 1)
         for c in range(n_chunks):
             r0 = c * CHUNK
             rows = slice(r0, r0 + CHUNK)
             sc = sc_ref.at[c]
-            state = sin_ref[q]
+            state = sin_ref[lax.div(q, n_sub), :, pl.ds(pl.multiple_of(lax.rem(q, n_sub) * QUAD, QUAD), QUAD)]
             if c > 0:
                 state = eexp_ref[0, 0:1, lanes] * state + st0_ref[0, :, lanes]
             ys = dot(c_ref[rows, :], state.astype(BF16)) * dot(wst_ref[0, rows, :], e_ref[:, lanes])
             y_ref[rows, lanes] = ys + eexp_ref[0, 7:8, lanes] * x_ref[rows, lanes].astype(F32)
             for hp in range(per_q // 2):
-                pl_lanes = pl.ds(pl.multiple_of(q * COLS + hp * pair, pair), pair)
+                pl_lanes = pl.ds(pl.multiple_of(q * QUAD + hp * pair, pair), pair)
                 xp = x_ref[rows, pl_lanes]
                 tops, bots = [], []
                 for hh in range(2):
@@ -455,28 +454,28 @@
         pairs = groups // 2
         bc_of = lambda i: lax.rem(cap(i), 2) * pairs + lax.div(cap(i), 2)
         x_blk = d_inner // gw
-        bc_blk = 2 * d_inner // COLS
-        cb_blk = d_inner // COLS
+        bc_blk = 2 * d_inner // BC_COLS
+        cb_blk = d_inner // BC_COLS
         proj = pl.pallas_call(
             functools.partial(proj_kernel, n_seq, groups),
             grid=(2 * groups,),
             in_specs=[pl.BlockSpec(memory_space=pl.ANY), full(HALO, d_model),
                       pl.BlockSpec((d_model, gw), lambda i: (0, jnp.where(i < groups, i + x_blk, i - groups))),
-                      pl.BlockSpec((d_model, COLS), lambda i: (0, bc_blk + bc_of(i))),
+                      pl.BlockSpec((d_model, BC_COLS), lambda i: (0, bc_blk + bc_of(i))),
                       pl.BlockSpec((4, gw), lambda i: (0, cap(i))), pl.BlockSpec((1, gw), lambda i: (0, cap(i))),
-                      pl.BlockSpec((4, COLS), lambda i: (0, cb_blk + bc_of(i))), pl.BlockSpec((1, COLS), lambda i: (0, cb_blk + bc_of(i))),
+                      pl.BlockSpec((4, BC_COLS), lambda i: (0, cb_blk + bc_of(i))), pl.BlockSpec((1, BC_COLS), lambda i: (0, cb_blk + bc_of(i))),
                       full(3, n_tok, 128),
                       pl.BlockSpec((1, n_tok, k3), lambda i: (cap(i), 0, 0)),
                       pl.BlockSpec((1, 8, gw), lambda i: (cap(i), 0, 0)),
                       full(groups, gw), full(k3, gw)],
             out_specs=[pl.BlockSpec((n_tok, gw), lambda i: (0, cap(i))),
-                       pl.BlockSpec((n_tok, COLS), lambda i: (0, bc_of(i))),
+                       pl.BlockSpec((n_tok, BC_COLS), lambda i: (0, bc_of(i))),
                        pl.BlockSpec((n_tok, gw), lambda i: (0, z_of(i))),
                        pl.BlockSpec((1, sdim, gw), lambda i: (cap(i), 0, 0)),
                        pl.BlockSpec(memory_space=pl.ANY)],
             out_shape=[sds((n_tok, d_inner), BF16), sds((n_tok, conv_dim - d_inner), BF16), sds((n_tok, d_inner), BF16),
                        sds((groups, sdim, gw), F32), sds((pieces, sdim, COLS), F32)],
-            scratch_shapes=[VMEM((n_tok + HALO, d_model), BF16), VMEM((n_tok + HALO, COLS), F32),
+            scratch_shapes=[VMEM((n_tok + HALO, d_model), BF16), VMEM((2, n_tok + HALO, COLS), F32), VMEM((n_tok + HALO, BC_COLS), F32),
                             VMEM((4, sdim, n_tok), BF16), VMEM((pieces, sdim, COLS), F32),
                             VMEM((pieces, sdim, COLS), F32), VMEM((pieces, sdim, COLS), F32), VMEM((groups, gw), F32),
                             pltpu.SemaphoreType.DMA((pieces,)), pltpu.SemaphoreType.DMA((pieces,)),

time: 212 us -> 196 us (0.925)
  Pallas kernels: 212 us -> 195 us
    pallas_call x1, Pallas kernels: 135 us -> 119 us  [layer_shard(): proj(x, tail, w_in, w_in, conv_w, conv_b[None], conv_w, conv_b[None], mas...]
where the time goes in v3:
time: 196 us; the launch traced here: 195 us
  Pallas kernels  195 us (99%)
    pallas_call x1, Pallas kernels, layer_shard(): proj(x, tail, w_in, w_in, conv_w, conv_b[None], conv_w, conv_b[None], mas...  119 us
    pallas_call x1, Pallas kernels, layer_shard(): finish(xc, z, bc, bc, ai, ajt, wst3, segc, segr, s_in, st0, eexp, expand,...  67.7 us
    pallas_call x1, Pallas kernels, layer_shard(): prep(x, w_in, dt_bias[None], a_log[None], d_skip[None], doc_start[None])  8.14 us

profile of v3, /device:TPU:21, one launch (start us, length us, event | category | flops | bytes accessed | tf_op | source)
XLA Modules:
  0.0 194.9 jit_solution(6761275050411965924)
XLA Ops:
  0.0 8.1 %prep.1 = (f32[512,128]{1,0:T(8,128)}, f32[128,512]{1,0:T(8,128)}, bf16[8,512,48]{2,1,0:T(8,128)(2,1)}, bf16[8,512,48]{2,1,0:T(8,128)(2,1)}, f32[8,8,1024]{2,1,0...) custom-call(bf16[512,4096]{1,0:T(8,128)(2,1)} %x_hbm.1, ...), custom_call_target="tpu_custom_call" | custom-call | tf_op jit(solution)/shard_map/prep/pallas_call | solution.py:449
  8.1 119.0 %proj.1 = (bf16[512,8192]{1,0:T(8,128)(2,1)}, bf16[512,2048]{1,0:T(8,128)(2,1)}, bf16[512,8192]{1,0:T(8,128)(2,1)}, f32[8,128,1024]{2,1,0:T(8,128)}, f32[16,128,512]{2,1,0:T(8,128)}) custom-call(bf16[512,4096]{1,0:T(8,128)(2,1)} %x_hbm.1, bf16[16,4096]{1,0:T(8,128)(2,1)} %get-tuple-element.21.tail_ref, bf16[4096,18560]{1,0:T(8,128)(2,1)} %wbc_ref.1, ...), custom_call_target="tpu_custom_call" | custom-call | tf_op jit(solution)/shard_map/proj/pallas_call | solution.py:487
  127.2 67.7 %finish.1 = bf16[512,4096]{1,0:T(8,128)(2,1)} custom-call(bf16[512,8192]{1,0:T(8,128)(2,1)} %get-tuple-element.27.x_ref, bf16[512,8192]{1,0:T(8,128)(2,1)} %get-tuple-element.28.z_ref, bf16[512,2048]{1,0:T(8,128)(2,1)} %get-tuple-element.29.b_ref.c_ref, bf16[512,2048]{1,0:T(8,128)(2,1)} %get-tuple-element.29.b_ref.c_ref, ...), custom_call_target="tpu_custom_call" | custom-call | tf_op jit(solution)/shard_map/finish/pallas_call | solution.py:507
